TPU v7x, 16 devices: a 4x2x1 block of a 4x4x8 slice. The times are simulated.
16 devices in a mesh: dp: 2 (over y, z), fsdp: 8 (over x, core).
Axes of the slice: x: 4, y: 2, z: 1, core: 2. Of those that a mesh axis runs over, the one named last changes fastest.
The devices are a block of a 4x4x8 slice.
Arguments:
- tokens: bfloat16 [32, 256, 2048], P(('dp', 'fsdp')), parts along dimension 0
- w_query: bfloat16 [2, 2048, 2048], P(None, 'fsdp')
- w_key: bfloat16 [2, 2048, 2048], P(None, 'fsdp')
- w_value: bfloat16 [2, 2048, 2048], P(None, 'fsdp')
- w_out: bfloat16 [2, 2048, 2048], P(None, 'fsdp')
- w_gate: bfloat16 [2, 2048, 8192], P(None, 'fsdp')
- w_up: bfloat16 [2, 2048, 8192], P(None, 'fsdp')
- w_down: bfloat16 [2, 8192, 2048], P(None, 'fsdp')
- g_query: bfloat16 [2, 2048], P(None, 'fsdp')
- g_key: bfloat16 [2, 2048], P(None, 'fsdp')
- g_attn: bfloat16 [2, 2048], P(None, 'fsdp')
- g_mlp: bfloat16 [2, 2048], P(None, 'fsdp')
Outputs:
- output: bfloat16 [32, 256, 2048], P(('dp', 'fsdp')), parts along dimension 0
There are 2 independent parts. A program takes and returns all parts, laid end to end along the dimension named above; an argument that names none is the same for every part.
All inputs are finite; a program needn't handle non-finite values.
Results may differ from a plain program's by a relative error of at most 0.02.
Values are sent between devices in bfloat16 or wider.
A program may use at most 768 MiB of HBM per device.

v0:
```python
import jax
import jax.numpy as jnp
from jax import lax
from jax.sharding import PartitionSpec as P

HEAD_DIM = 128
EPS = 1e-6
THETA = 500000.0
Q_BLOCK = 256


def rms_norm(values, gain_vec):
    mean_sq = jnp.mean(values * values, axis=-1, keepdims=True)
    return values * lax.rsqrt(mean_sq + EPS) * gain_vec.astype(jnp.float32)


def rope_tables(seq_len):
    positions = jnp.arange(seq_len, dtype=jnp.float32)
    inv_freq = THETA ** (-2.0 * jnp.arange(HEAD_DIM // 2, dtype=jnp.float32) / HEAD_DIM)
    angles = positions[:, None] * inv_freq[None, :]
    return jnp.cos(angles), jnp.sin(angles)


def apply_rope(values, cos_tab, sin_tab):
    half_dim = values.shape[-1] // 2
    first = values[..., :half_dim]
    second = values[..., half_dim:]
    cos_b = cos_tab[:, None, :]
    sin_b = sin_tab[:, None, :]
    return jnp.concatenate([first * cos_b - second * sin_b, second * cos_b + first * sin_b], axis=-1)


def dot_bf16(left, right):
    return jnp.dot(left, right, preferred_element_type=jnp.float32).astype(jnp.bfloat16)


def causal_attention(q_rot, k_rot, v_heads):
    seq_len = q_rot.shape[1]
    q_block = min(seq_len, Q_BLOCK)
    att_scale = HEAD_DIM ** -0.5
    pieces = []
    for block_idx in range(seq_len // q_block):
        start = block_idx * q_block
        stop = start + q_block
        scores = jnp.einsum('bqhd,bkhd->bhqk', q_rot[:, start:stop], k_rot[:, :stop], preferred_element_type=jnp.float32) * att_scale
        q_pos = start + jnp.arange(q_block)
        causal = q_pos[:, None] >= jnp.arange(stop)[None, :]
        scores = jnp.where(causal, scores, -jnp.inf)
        probs = jax.nn.softmax(scores, axis=-1).astype(jnp.bfloat16)
        pieces.append(jnp.einsum('bhqk,bkhd->bqhd', probs, v_heads[:, :stop], preferred_element_type=jnp.float32).astype(jnp.bfloat16))
    return jnp.concatenate(pieces, axis=1)


def layer_forward(x_loc, layer_w, cos_tab, sin_tab):
    w_query, w_key, w_value, w_out, w_gate, w_up, w_down, g_query, g_key, g_attn, g_mlp = layer_w
    n_batch, seq_len, width = x_loc.shape
    n_heads = width // HEAD_DIM
    flat_x = x_loc.reshape(n_batch * seq_len, width)

    def norm_rope(lin_vals, gain_vec):
        normed = rms_norm(lin_vals.astype(jnp.float32), gain_vec).reshape(n_batch, seq_len, n_heads, HEAD_DIM)
        return apply_rope(normed, cos_tab, sin_tab).astype(jnp.bfloat16)

    q_rot = norm_rope(dot_bf16(flat_x, w_query), g_query)
    k_rot = norm_rope(dot_bf16(flat_x, w_key), g_key)
    v_heads = dot_bf16(flat_x, w_value).reshape(n_batch, seq_len, n_heads, HEAD_DIM)
    attn_out = causal_attention(q_rot, k_rot, v_heads).reshape(n_batch * seq_len, width)
    a_lin = dot_bf16(attn_out, w_out)
    hidden = (flat_x.astype(jnp.float32) + rms_norm(a_lin.astype(jnp.float32), g_attn)).astype(jnp.bfloat16)
    gate_proj = dot_bf16(hidden, w_gate)
    up_proj = dot_bf16(hidden, w_up)
    gated = (jax.nn.silu(gate_proj.astype(jnp.float32)) * up_proj.astype(jnp.float32)).astype(jnp.bfloat16)
    down_proj = dot_bf16(gated, w_down)
    result = (hidden.astype(jnp.float32) + rms_norm(down_proj.astype(jnp.float32), g_mlp)).astype(jnp.bfloat16)
    return result.reshape(n_batch, seq_len, width)


def solution(mesh):
    def gather_rows(arr_w, layer_idx):
        return lax.all_gather(arr_w[layer_idx], 'fsdp', axis=0, tiled=True)

    def local_fn(tokens, weights):
        cos_tab, sin_tab = rope_tables(tokens.shape[1])
        current = tokens
        for layer_idx in range(weights[0].shape[0]):
            layer_w = tuple(gather_rows(arr_w, layer_idx) for arr_w in weights)
            current = layer_forward(current, layer_w, cos_tab, sin_tab)
        return current

    mapped = jax.shard_map(local_fn, mesh=mesh, in_specs=(P(('dp', 'fsdp')), P(None, 'fsdp')), out_specs=P(('dp', 'fsdp')), check_vma=False)

    def run(tokens, w_query, w_key, w_value, w_out, w_gate, w_up, w_down, g_query, g_key, g_attn, g_mlp):
        return mapped(tokens, (w_query, w_key, w_value, w_out, w_gate, w_up, w_down, g_query, g_key, g_attn, g_mlp))

    return run
```

profile of v0, /device:TPU:112, one launch (start us, length us, event | category | flops | bytes accessed | tf_op | source)
XLA Modules:
  0.0 1353.6 jit_solution(15837098665186506997)
XLA Ops:
  40.2 24.3 %all-gather.2 = bf16[1,2048]{1,0:T(2,128)(2,1)S(1)} all-gather(bf16[1,256]{1,0:T(2,128)(2,1)S(1)} %get-tuple-element.46), channel_id=4, replica_groups=mesh['dp'=2,'fsdp'=8] {'fsdp'}, dimensions={1}, use_global_device_ids=true | all-gather | bytes 4608 | tf_op jit(solution)/shard_map/all_gather | solution.py:80
  64.6 21.2 %all-gather.4 = bf16[1,2048]{1,0:T(2,128)(2,1)S(1)} all-gather(bf16[1,256]{1,0:T(2,128)(2,1)S(1)} %get-tuple-element.44), channel_id=6, replica_groups=mesh['dp'=2,'fsdp'=8] {'fsdp'}, dimensions={1}, use_global_device_ids=true | all-gather | bytes 4608 | tf_op jit(solution)/shard_map/all_gather | solution.py:80
  85.8 23.1 %all-gather.6 = bf16[1,2048]{1,0:T(2,128)(2,1)S(1)} all-gather(bf16[1,256]{1,0:T(2,128)(2,1)S(1)} %get-tuple-element.42), channel_id=8, replica_groups=mesh['dp'=2,'fsdp'=8] {'fsdp'}, dimensions={1}, use_global_device_ids=true | all-gather | bytes 4608 | tf_op jit(solution)/shard_map/all_gather | solution.py:80
  108.9 21.2 %all-gather.10 = bf16[1,2048]{1,0:T(2,128)(2,1)S(1)} all-gather(bf16[1,256]{1,0:T(2,128)(2,1)S(1)} %get-tuple-element.40), channel_id=12, replica_groups=mesh['dp'=2,'fsdp'=8] {'fsdp'}, dimensions={1}, use_global_device_ids=true | all-gather | bytes 4608 | tf_op jit(solution)/shard_map/all_gather | solution.py:80
  130.6 23.1 %all-gather.13 = bf16[1,2048]{1,0:T(2,128)(2,1)S(1)} all-gather(bf16[1,256]{1,0:T(2,128)(2,1)S(1)} %get-tuple-element.45), channel_id=15, replica_groups=mesh['dp'=2,'fsdp'=8] {'fsdp'}, dimensions={1}, use_global_device_ids=true | all-gather | bytes 4608 | tf_op jit(solution)/shard_map/all_gather | solution.py:80
  154.3 21.1 %all-gather.15 = bf16[1,2048]{1,0:T(2,128)(2,1)S(1)} all-gather(bf16[1,256]{1,0:T(2,128)(2,1)S(1)} %get-tuple-element.43), channel_id=17, replica_groups=mesh['dp'=2,'fsdp'=8] {'fsdp'}, dimensions={1}, use_global_device_ids=true | all-gather | bytes 4608 | tf_op jit(solution)/shard_map/all_gather | solution.py:80
  176.0 23.1 %all-gather.17 = bf16[1,2048]{1,0:T(2,128)(2,1)S(1)} all-gather(bf16[1,256]{1,0:T(2,128)(2,1)S(1)} %get-tuple-element.41), channel_id=19, replica_groups=mesh['dp'=2,'fsdp'=8] {'fsdp'}, dimensions={1}, use_global_device_ids=true | all-gather | bytes 4608 | tf_op jit(solution)/shard_map/all_gather | solution.py:80
  199.7 21.6 %all-gather.21 = bf16[1,2048]{1,0:T(2,128)(2,1)S(1)} all-gather(bf16[1,256]{1,0:T(2,128)(2,1)S(1)} %get-tuple-element.39), channel_id=23, replica_groups=mesh['dp'=2,'fsdp'=8] {'fsdp'}, dimensions={1}, use_global_device_ids=true | all-gather | bytes 4608 | tf_op jit(solution)/shard_map/all_gather | solution.py:80
  222.5 8.3 fusion.58
  234.2 8.2 fusion.61
  245.9 8.2 fusion.163
  279.2 8.4 fusion.64
  288.8 66.6 %all-gather.45.cloned.1.call-done = bf16[1,2048,8192]{2,1,0:T(8,128)(2,1)} async-done(((bf16[1,256,8192]{2,1,0:T(8,128)(2,1)}), bf16[1,2048,8192]{2,1,0:T(8,128)(2,1)}) %all-gather.45.cloned.1.call-update) | async-done | bytes 33554448 | tf_op jit(solution)/shard_map/all_gather | solution.py:80
  355.4 25.6 %fusion.24 = bf16[512,8192]{1,0:T(8,128)(2,1)} fusion(bf16[512,2048]{1,0:T(8,128)(2,1)S(1)} %fusion.67, bf16[1,2048,8192]{2,1,0:T(8,128)(2,1)} %all-gather.45.cloned.1.call-done), kind=kOutput, calls=%fused_computation.28 | convolution fusion | flops 17184063488 | bytes 44040192 | tf_op jit(solution)/shard_map/dot_general | solution.py:34
  381.0 129.4 %all-gather.47.cloned.1.call-done = bf16[1,2048,8192]{2,1,0:T(8,128)(2,1)} async-done(((bf16[1,256,8192]{2,1,0:T(8,128)(2,1)}), bf16[1,2048,8192]{2,1,0:T(8,128)(2,1)}) %all-gather.47.cloned.1.call-update) | async-done | bytes 33554448 | tf_op jit(solution)/shard_map/all_gather | solution.py:80
  510.5 25.6 %fusion.122.clone.4 = bf16[512,8192]{1,0:T(8,128)(2,1)} fusion(bf16[512,8192]{1,0:T(8,128)(2,1)} %fusion.24, bf16[512,2048]{1,0:T(8,128)(2,1)S(1)} %fusion.67, bf16[1,2048,8192]{2,1,0:T(8,128)(2,1)} %all-gather.47.cloned.1.call-done), kind=kOutput, calls=%fused_computation.27.clone.clone.clone.clone.clone.clone.1 | convolution fusion | flops 17217617920 | bytes 52428800 | tf_op jit(solution)/shard_map/dot_general | solution.py:34
  536.1 129.6 %all-gather.49.cloned.1.call-done = bf16[1,8192,2048]{2,1,0:T(8,128)(2,1)} async-done(((bf16[1,1024,2048]{2,1,0:T(8,128)(2,1)}), bf16[1,8192,2048]{2,1,0:T(8,128)(2,1)}) %all-gather.49.cloned.1.call-update) | async-done | bytes 33554448 | tf_op jit(solution)/shard_map/all_gather | solution.py:80
  665.7 24.6 %fusion.68 = (f32[512]{0:T(512)S(1)}, bf16[512,2048]{1,0:T(8,128)(2,1)S(1)}) fusion(bf16[1,8192,2048]{2,1,0:T(8,128)(2,1)} %all-gather.49.cloned.1.call-done, bf16[512,8192]{1,0:T(8,128)(2,1)} %fusion.122.clone.4), kind=kOutput, calls=%fused_computation.84 | convolution fusion | flops 17184063488 | bytes 44042240 | tf_op jit(solution)/shard_map/dot_general | solution.py:34
  691.6 22.1 %all-gather.53.cloned.1.call-done = bf16[1,2048,2048]{2,1,0:T(8,128)(2,1)} async-done(((bf16[1,256,2048]{2,1,0:T(8,128)(2,1)}), bf16[1,2048,2048]{2,1,0:T(8,128)(2,1)}) %all-gather.53.cloned.1.call-update) | async-done | bytes 8388624 | tf_op jit(solution)/shard_map/all_gather | solution.py:80
  713.7 8.2 fusion.72
  725.4 35.5 %all-gather.55.cloned.1.call-done = bf16[1,2048,2048]{2,1,0:T(8,128)(2,1)} async-done(((bf16[1,256,2048]{2,1,0:T(8,128)(2,1)}), bf16[1,2048,2048]{2,1,0:T(8,128)(2,1)}) %all-gather.55.cloned.1.call-update) | async-done | bytes 8388624 | tf_op jit(solution)/shard_map/all_gather | solution.py:80
  761.0 8.2 fusion.75
  772.6 35.5 %all-gather.51.cloned.1.call-done = bf16[1,2048,2048]{2,1,0:T(8,128)(2,1)} async-done(((bf16[1,256,2048]{2,1,0:T(8,128)(2,1)}), bf16[1,2048,2048]{2,1,0:T(8,128)(2,1)}) %all-gather.51.cloned.1.call-update) | async-done | bytes 8388624 | tf_op jit(solution)/shard_map/all_gather | solution.py:80
  808.1 8.2 fusion.160
  839.1 16.3 %all-gather.57.cloned.1.call-done = bf16[1,2048,2048]{2,1,0:T(8,128)(2,1)} async-done(((bf16[1,256,2048]{2,1,0:T(8,128)(2,1)}), bf16[1,2048,2048]{2,1,0:T(8,128)(2,1)}) %all-gather.57.cloned.1.call-update) | async-done | bytes 8388624 | tf_op jit(solution)/shard_map/all_gather | solution.py:80
  855.4 8.6 fusion.78
  865.2 144.6 %all-gather.59.cloned.1.call-done = bf16[1,2048,8192]{2,1,0:T(8,128)(2,1)} async-done(((bf16[1,256,8192]{2,1,0:T(8,128)(2,1)}), bf16[1,2048,8192]{2,1,0:T(8,128)(2,1)}) %all-gather.59.cloned.1.call-update) | async-done | bytes 33554448 | tf_op jit(solution)/shard_map/all_gather | solution.py:80
  1009.8 25.5 %fusion.30 = bf16[512,8192]{1,0:T(8,128)(2,1)} fusion(bf16[512,2048]{1,0:T(8,128)(2,1)S(1)} %fusion.81, bf16[1,2048,8192]{2,1,0:T(8,128)(2,1)} %all-gather.59.cloned.1.call-done), kind=kOutput, calls=%fused_computation.30 | convolution fusion | flops 17184063488 | bytes 44040192 | tf_op jit(solution)/shard_map/dot_general | solution.py:34
  1035.3 129.7 %all-gather.61.cloned.1.call-done = bf16[1,2048,8192]{2,1,0:T(8,128)(2,1)} async-done(((bf16[1,256,8192]{2,1,0:T(8,128)(2,1)}), bf16[1,2048,8192]{2,1,0:T(8,128)(2,1)}) %all-gather.61.cloned.1.call-update) | async-done | bytes 33554448 | tf_op jit(solution)/shard_map/all_gather | solution.py:80
  1165.0 25.9 %fusion.131.clone.2 = bf16[512,8192]{1,0:T(8,128)(2,1)} fusion(bf16[512,8192]{1,0:T(8,128)(2,1)} %fusion.30, bf16[512,2048]{1,0:T(8,128)(2,1)S(1)} %fusion.81, bf16[1,2048,8192]{2,1,0:T(8,128)(2,1)} %all-gather.61.cloned.1.call-done), kind=kOutput, calls=%fused_computation.26.clone.clone.clone.clone.clone.clone | convolution fusion | flops 17217617920 | bytes 52428800 | tf_op jit(solution)/shard_map/dot_general | solution.py:34
  1191.0 129.1 %all-gather.63.cloned.1.call-done = bf16[1,8192,2048]{2,1,0:T(8,128)(2,1)} async-done(((bf16[1,1024,2048]{2,1,0:T(8,128)(2,1)}), bf16[1,8192,2048]{2,1,0:T(8,128)(2,1)}) %all-gather.63.cloned.1.call-update) | async-done | bytes 33554448 | tf_op jit(solution)/shard_map/all_gather | solution.py:80
  1320.1 24.1 %fusion.82 = (f32[512]{0:T(512)S(1)}, bf16[512,2048]{1,0:T(8,128)(2,1)S(1)}) fusion(bf16[1,8192,2048]{2,1,0:T(8,128)(2,1)} %all-gather.63.cloned.1.call-done, bf16[512,8192]{1,0:T(8,128)(2,1)} %fusion.131.clone.2), kind=kOutput, calls=%fused_computation.98 | convolution fusion | flops 17184063488 | bytes 44042240 | tf_op jit(solution)/shard_map/dot_general | solution.py:34
  (147 shorter events, 104.3 us)
Async XLA Ops:
  6.5 215.9 %all-gather.39.cloned.1.call-start = ((), (), s32[]{:S(2)}) async-start(), calls=%async_computation.1 | async-start | bytes 9437184 | tf_op jit(solution)/shard_map/all_gather | solution.py:80
  9.9 224.3 %all-gather.41.cloned.1.call-start = ((), (), s32[]{:S(2)}) async-start(), calls=%async_computation.2 | async-start | bytes 9437184 | tf_op jit(solution)/shard_map/all_gather | solution.py:80
  11.5 234.3 %all-gather.37.cloned.1.call-start = ((), (), s32[]{:S(2)}) async-start(), calls=%async_computation | async-start | bytes 9437184 | tf_op jit(solution)/shard_map/all_gather | solution.py:80
  14.9 264.3 %all-gather.43.cloned.1.call-start = ((), (), s32[]{:S(2)}) async-start(), calls=%async_computation.3 | async-start | bytes 9437184 | tf_op jit(solution)/shard_map/all_gather | solution.py:80
  16.5 338.9 %all-gather.45.cloned.1.call-start = ((), (), s32[]{:S(2)}) async-start(), calls=%async_computation.4 | async-start | bytes 37748736 | tf_op jit(solution)/shard_map/all_gather | solution.py:80
  22.7 487.8 %all-gather.47.cloned.1.call-start = ((), (), s32[]{:S(2)}) async-start(), calls=%async_computation.5 | async-start | bytes 37748736 | tf_op jit(solution)/shard_map/all_gather | solution.py:80
  28.8 636.9 %all-gather.49.cloned.1.call-start = ((), (), s32[]{:S(2)}) async-start(), calls=%async_computation.6 | async-start | bytes 37748736 | tf_op jit(solution)/shard_map/all_gather | solution.py:80
  35.0 678.6 %all-gather.53.cloned.1.call-start = ((), (), s32[]{:S(2)}) async-start(), calls=%async_computation.8 | async-start | bytes 9437184 | tf_op jit(solution)/shard_map/all_gather | solution.py:80
  35.8 725.1 %all-gather.55.cloned.1.call-start = ((), (), s32[]{:S(2)}) async-start(), calls=%async_computation.9 | async-start | bytes 9437184 | tf_op jit(solution)/shard_map/all_gather | solution.py:80
  36.6 771.5 %all-gather.51.cloned.1.call-start = ((), (), s32[]{:S(2)}) async-start(), calls=%async_computation.7 | async-start | bytes 9437184 | tf_op jit(solution)/shard_map/all_gather | solution.py:80
  37.3 818.1 %all-gather.57.cloned.1.call-start = ((), (), s32[]{:S(2)}) async-start(), calls=%async_computation.10 | async-start | bytes 9437184 | tf_op jit(solution)/shard_map/all_gather | solution.py:80
  38.1 971.7 %all-gather.59.cloned.1.call-start = ((), (), s32[]{:S(2)}) async-start(), calls=%async_computation.11 | async-start | bytes 37748736 | tf_op jit(solution)/shard_map/all_gather | solution.py:80
  38.7 1126.3 %all-gather.61.cloned.1.call-start = ((), (), s32[]{:S(2)}) async-start(), calls=%async_computation.12 | async-start | bytes 37748736 | tf_op jit(solution)/shard_map/all_gather | solution.py:80
  38.8 25.7 %copy-start.26 = (bf16[2,256]{1,0:T(2,128)(2,1)S(1)}, bf16[2,256]{1,0:T(2,128)(2,1)}, u32[]{:S(2)}) copy-start(bf16[2,256]{1,0:T(2,128)(2,1)} %param.21) | copy-start | bytes 3076
  38.8 47.0 %copy-start.27 = (bf16[2,256]{1,0:T(2,128)(2,1)S(1)}, bf16[2,256]{1,0:T(2,128)(2,1)}, u32[]{:S(2)}) copy-start(bf16[2,256]{1,0:T(2,128)(2,1)} %param.22) | copy-start | bytes 3076
  38.8 70.0 %copy-start.28 = (bf16[2,256]{1,0:T(2,128)(2,1)S(1)}, bf16[2,256]{1,0:T(2,128)(2,1)}, u32[]{:S(2)}) copy-start(bf16[2,256]{1,0:T(2,128)(2,1)} %param.23) | copy-start | bytes 3076
  38.8 183.6 %copy-start.8 = (bf16[2,256,2048]{2,1,0:T(8,128)(2,1)S(1)}, bf16[2,256,2048]{2,1,0:T(8,128)(2,1)}, u32[]{:S(2)}) copy-start(bf16[2,256,2048]{2,1,0:T(8,128)(2,1)} %param.12) | copy-start | bytes 6291460
  39.5 1280.6 %all-gather.63.cloned.1.call-start = ((), (), s32[]{:S(2)}) async-start(), calls=%async_computation.13 | async-start | bytes 37748736 | tf_op jit(solution)/shard_map/all_gather | solution.py:80
  221.9 48.8 %copy-start.18 = (pred[256,256]{0,1:T(8,128)(4,1)}, pred[256,256]{0,1:T(8,128)(4,1)S(1)}, u32[]{:S(2)}) copy-start(pred[256,256]{0,1:T(8,128)(4,1)S(1)} %iota_compare_fusion) | copy-start | bytes 196612
  222.4 38.7 %copy-start.14 = (f32[256,64]{1,0:T(8,128)}, f32[256,64]{1,0:T(8,128)S(1)}, u32[]{:S(2)}) copy-start(f32[256,64]{1,0:T(8,128)S(1)} %get-tuple-element.47) | copy-start | bytes 196612
  222.4 38.7 %copy-start.16 = (f32[256,64]{1,0:T(8,128)}, f32[256,64]{1,0:T(8,128)S(1)}, u32[]{:S(2)}) copy-start(f32[256,64]{1,0:T(8,128)S(1)} %get-tuple-element.48) | copy-start | bytes 196612
  245.9 10.2 copy-start.3
  279.2 8.5 copy-start.9
  288.8 221.7 %copy-start.6 = (bf16[512,2048]{1,0:T(8,128)(2,1)}, bf16[512,2048]{1,0:T(8,128)(2,1)S(1)}, u32[]{:S(2)}) copy-start(bf16[512,2048]{1,0:T(8,128)(2,1)S(1)} %fusion.67) | copy-start | bytes 6291460
  536.1 154.3 %copy-start.24 = (f32[1,2048]{1,0:T(1,128)S(1)}, f32[1,2048]{1,0:T(1,128)}, u32[]{:S(2)}) copy-start(f32[1,2048]{1,0:T(1,128)} %convert_element_type.207) | copy-start | bytes 24580
  665.7 24.7 %copy-start.7 = (bf16[512,2048]{1,0:T(8,128)(2,1)S(1)}, bf16[512,2048]{1,0:T(8,128)(2,1)}, u32[]{:S(2)}) copy-start(bf16[512,2048]{1,0:T(8,128)(2,1)} %copy-done.6) | copy-start | bytes 6291460
  691.6 116.5 %copy-start.4 = (bf16[512,2048]{1,0:T(8,128)(2,1)}, bf16[512,2048]{1,0:T(8,128)(2,1)S(1)}, u32[]{:S(2)}) copy-start(bf16[512,2048]{1,0:T(8,128)(2,1)S(1)} %fusion.71) | copy-start | bytes 6291460
  691.6 30.3 %copy-start.23 = (f32[1,2048]{1,0:T(1,128)S(1)}, f32[1,2048]{1,0:T(1,128)}, u32[]{:S(2)}) copy-start(f32[1,2048]{1,0:T(1,128)} %convert_element_type.208) | copy-start | bytes 24580
  725.4 43.8 %copy-start.22 = (f32[1,2048]{1,0:T(1,128)S(1)}, f32[1,2048]{1,0:T(1,128)}, u32[]{:S(2)}) copy-start(f32[1,2048]{1,0:T(1,128)} %convert_element_type.209) | copy-start | bytes 24580
  855.4 8.6 copy-start.5
  855.4 8.6 copy-start.21
  1191.0 153.2 %copy-start.20 = (f32[1,2048]{1,0:T(1,128)S(1)}, f32[1,2048]{1,0:T(1,128)}, u32[]{:S(2)}) copy-start(f32[1,2048]{1,0:T(1,128)} %convert_element_type.211) | copy-start | bytes 24580
  (11 other events, 26.5 us)
Sparse Core Ops, SparseCore 0:
  10.0 48.3 all-gather.38
  60.1 45.9 all-gather.40
  107.7 45.8 all-gather.36
  155.1 45.9 all-gather.42
  202.5 152.9 all-gather.44
  356.9 153.5 all-gather.46
  512.1 153.5 all-gather.48
  667.3 46.3 all-gather.52
  715.3 45.6 all-gather.54
  762.4 45.6 all-gather.50
  809.7 45.6 all-gather.56
  856.9 152.9 all-gather.58
  1011.4 153.5 all-gather.60
  1166.5 153.5 all-gather.62
where the time goes:
time: 1360 us; the launch traced here: 1350 us
  waiting for transfers between devices  843 us (62%)
  matrix products  228 us (17%)
  blocking collectives  179 us (13%)
  local copies, waits for them, and re-layouts  59.9 us (4%)
  other arithmetic  28.4 us (2%)
  between operations  14.4 us (1%)
    all_gather x14, waiting for transfers between devices, gather_rows(): return lax.all_gather(arr_w[layer_idx], 'fsdp', axis=0, tiled=True)  839 us
    dot_general x14, matrix products, dot_bf16(): jnp.dot(left, right, preferred_element_type=jnp.float32)  218 us
    all_gather x8, blocking collectives, gather_rows(): return lax.all_gather(arr_w[layer_idx], 'fsdp', axis=0, tiled=True)  179 us
    slice x11, local copies, waits for them, and re-layouts, gather_rows(): return lax.all_gather(arr_w[layer_idx], 'fsdp', axis=0, tiled=True)  27.6 us
  transfers between devices with their start and end apart: 14, of which 10 were waited for; matrix products, arithmetic and copies ran while one was open for 21% of the time, Pallas kernels for 0%

commit v1 on v0

v1 whole, which is shorter than its diff:
```python
import jax
import jax.numpy as jnp
from jax import lax
from jax.sharding import PartitionSpec as P

HEAD_DIM = 128
EPS = 1e-6
THETA = 500000.0


def rope_tables(seq_len):
    positions = jnp.arange(seq_len, dtype=jnp.float32)
    inv_freq = THETA ** (-2.0 * jnp.arange(HEAD_DIM // 2, dtype=jnp.float32) / HEAD_DIM)
    angles = positions[:, None] * inv_freq[None, :]
    return jnp.cos(angles), jnp.sin(angles)


def apply_rope(values, cos_tab, sin_tab):
    half_dim = values.shape[-1] // 2
    first = values[..., :half_dim]
    second = values[..., half_dim:]
    cos_b = cos_tab[:, None, :]
    sin_b = sin_tab[:, None, :]
    return jnp.concatenate([first * cos_b - second * sin_b, second * cos_b + first * sin_b], axis=-1)


def dot_f32(left, right):
    return jnp.dot(left, right, preferred_element_type=jnp.float32)


def dot_bf16(left, right):
    return dot_f32(left, right).astype(jnp.bfloat16)


def causal_attention(q_rot, k_rot, v_heads):
    seq_len = q_rot.shape[1]
    scores = jnp.einsum('bqhd,bkhd->bhqk', q_rot, k_rot, preferred_element_type=jnp.float32) * HEAD_DIM ** -0.5
    pos = jnp.arange(seq_len)
    scores = jnp.where(pos[:, None] >= pos[None, :], scores, -jnp.inf)
    probs = jax.nn.softmax(scores, axis=-1).astype(jnp.bfloat16)
    return jnp.einsum('bhqk,bkhd->bqhd', probs, v_heads, preferred_element_type=jnp.float32).astype(jnp.bfloat16)


def residual_norm(res, lin, gain):
    lin = lin.astype(jnp.bfloat16).astype(jnp.float32)
    mean_sq = jnp.mean(lin * lin, axis=-1, keepdims=True)
    return (res.astype(jnp.float32) + lin * lax.rsqrt(mean_sq + EPS) * gain).astype(jnp.bfloat16)


def solution(mesh):
    n_dp = mesh.shape['dp']
    n_fsdp = mesh.shape['fsdp']
    pairs = [(g, g ^ 1) for g in range(n_dp)]

    def swap(arr):
        return lax.ppermute(arr, 'dp', pairs)

    def gather(arr):
        return lax.all_gather(arr, 'fsdp', axis=0, tiled=True)

    def local_fn(tokens, weights):
        w_query, w_key, w_value, w_out, w_gate, w_up, w_down, g_query, g_key, g_attn, g_mlp = weights
        part = lax.rem(lax.axis_index('dp'), 2)
        n_layers, rows, width = w_query.shape
        ff = w_gate.shape[2]
        down_rows = w_down.shape[1]
        n_seq, seq_len, _ = tokens.shape
        n_tok = n_seq * seq_len
        half = width // 2
        n_heads = half // HEAD_DIM
        cos_tab, sin_tab = rope_tables(seq_len)

        def my_half(arr, axis):
            size = arr.shape[axis] // 2
            return lax.dynamic_slice_in_dim(arr, part * size, size, axis)

        gains = jnp.concatenate([g_query, g_key, g_attn, g_mlp], axis=0)
        gains = lax.all_gather(gains, 'fsdp', axis=1, tiled=True).astype(jnp.float32)

        def gain(kind, layer):
            return gains[kind * n_layers + layer]

        full_w = []
        for layer in range(n_layers):
            qkv = jnp.concatenate([my_half(w[layer], 1) for w in (w_query, w_key, w_value)], axis=1)
            gate_up = jnp.concatenate([
                my_half(w[layer].reshape(rows, n_fsdp, ff // n_fsdp), 2).reshape(rows, ff // 2)
                for w in (w_gate, w_up)], axis=1)
            down = my_half(w_down[layer], 0)
            full_w.append([gather(qkv), gather(w_out[layer]), gather(gate_up),
                           [gather(down[:, :half]), gather(down[:, half:])] if layer == n_layers - 1 else [gather(down)]])

        own = tokens.reshape(n_tok, width)
        for layer in range(n_layers):
            qkv_w, out_w, gu_w, down_w = full_w[layer]
            both = jnp.concatenate([own, swap(own)], axis=0)
            lin = dot_bf16(both, qkv_w)
            q_lin = lin[:, :half].astype(jnp.float32)
            k_lin = lin[:, half:2 * half].astype(jnp.float32)
            v_heads = lin[:, 2 * half:].reshape(2 * n_seq, seq_len, n_heads, HEAD_DIM)
            stats = jnp.stack([jnp.sum(q_lin * q_lin, axis=-1), jnp.sum(k_lin * k_lin, axis=-1)])
            other = jnp.roll(swap(stats), n_tok, axis=1)
            inv = lax.rsqrt((stats + other) / width + EPS)

            def norm_rope(vals, inv_rms, gain_vec):
                normed = vals * inv_rms[:, None] * gain_vec
                normed = normed.reshape(2 * n_seq, seq_len, n_heads, HEAD_DIM)
                return apply_rope(normed, cos_tab, sin_tab).astype(jnp.bfloat16)

            q_rot = norm_rope(q_lin, inv[0], my_half(gain(0, layer), 0))
            k_rot = norm_rope(k_lin, inv[1], my_half(gain(1, layer), 0))
            attn = causal_attention(q_rot, k_rot, v_heads).reshape(2 * n_tok, half)
            mine, theirs = attn[:n_tok], swap(attn[n_tok:])
            attn_own = jnp.where(part == 0, jnp.concatenate([mine, theirs], axis=1), jnp.concatenate([theirs, mine], axis=1))
            hidden = residual_norm(own, dot_bf16(attn_own, out_w), gain(2, layer))
            hidden_other = swap(hidden)

            def mlp_mid(hid):
                gate_up = dot_bf16(hid, gu_w)
                gate = gate_up[:, :ff // 2].astype(jnp.float32)
                up = gate_up[:, ff // 2:].astype(jnp.float32)
                return (jax.nn.silu(gate) * up).astype(jnp.bfloat16)

            mid_own = mlp_mid(hidden)
            mid_other = mlp_mid(hidden_other)
            sums = []
            for piece in down_w:
                theirs_sum = swap(dot_f32(mid_other, piece))
                sums.append(dot_f32(mid_own, piece) + theirs_sum)
            down_lin = jnp.concatenate(sums, axis=1) if len(sums) > 1 else sums[0]
            own = residual_norm(hidden, down_lin, gain(3, layer))
        return own.reshape(n_seq, seq_len, width)

    mapped = jax.shard_map(local_fn, mesh=mesh, in_specs=(P(('dp', 'fsdp')), P(None, 'fsdp')), out_specs=P(('dp', 'fsdp')), check_vma=False)

    def run(tokens, w_query, w_key, w_value, w_out, w_gate, w_up, w_down, g_query, g_key, g_attn, g_mlp):
        return mapped(tokens, (w_query, w_key, w_value, w_out, w_gate, w_up, w_down, g_query, g_key, g_attn, g_mlp))

    return run
```

time: 1360 us -> 817 us (0.60)
  waiting for transfers between devices: 843 us -> 405 us
  blocking collectives: 179 us -> 23.8 us
  local copies, waits for them, and re-layouts: 59.9 us -> 80.4 us
  starting transfers between devices: 0.82 us -> 17.3 us
    all_gather x14 -> x9, waiting for transfers between devices: 839 us -> 117 us  [gather(): return lax.all_gather(arr, 'fsdp', axis=0, tiled=True)]
    ppermute x0 -> x11, waiting for transfers between devices: none -> 287 us  [swap(): return lax.ppermute(arr, 'dp', pairs)]
    all_gather x8 -> x1, blocking collectives: 179 us -> 23.8 us  [local_fn(): lax.all_gather(gains, 'fsdp', axis=1, tiled=True).astype(jnp.float32)]
    unnamed x64 -> x82, local copies, waits for them, and re-layouts: 18.6 us -> 38.7 us
    ppermute x0 -> x11, starting transfers between devices: none -> 16.4 us  [swap(): return lax.ppermute(arr, 'dp', pairs)]
    slice x11 -> x19, local copies, waits for them, and re-layouts: 27.6 us -> 29.2 us  [the longest x2 10.7 us: local_fn(): w[layer].reshape(rows, n_fsdp, ff // n_fsdp)]
  transfers between devices with their start and end apart: 14 -> 20, of which waited for: 10 -> 12; matrix products, arithmetic and copies ran while one was open for 21% -> 41% of each run, Pallas kernels for 0% -> 0%
where the time goes in v1:
time: 817 us; the launch traced here: 812 us
  waiting for transfers between devices  405 us (50%)
  matrix products  235 us (29%)
  local copies, waits for them, and re-layouts  80.4 us (10%)
  other arithmetic  35.6 us (4%)
  blocking collectives  23.8 us (3%)
  starting transfers between devices  17.3 us (2%)
  between operations  14.2 us (2%)
    ppermute x11, waiting for transfers between devices, swap(): return lax.ppermute(arr, 'dp', pairs)  287 us
    dot_general x14, matrix products, dot_f32(): return jnp.dot(left, right, preferred_element_type=jnp.float32)  227 us
    all_gather x9, waiting for transfers between devices, gather(): return lax.all_gather(arr, 'fsdp', axis=0, tiled=True)  117 us
    unnamed x82, local copies, waits for them, and re-layouts  38.7 us
    all_gather x1, blocking collectives, local_fn(): lax.all_gather(gains, 'fsdp', axis=1, tiled=True).astype(jnp.float32)  23.8 us
    ppermute x11, starting transfers between devices, swap(): return lax.ppermute(arr, 'dp', pairs)  16.4 us
  transfers between devices with their start and end apart: 20, of which 12 were waited for; matrix products, arithmetic and copies ran while one was open for 41% of the time, Pallas kernels for 0%

profile of v1, /device:TPU:112, one launch (start us, length us, event | category | flops | bytes accessed | tf_op | source)
XLA Modules:
  0.0 811.6 jit_solution(5754420065019043498)
XLA Ops:
  23.3 6.3 copy.52
  29.7 5.6 fusion.148
  35.3 6.3 copy.54
  57.9 6.7 copy.61
  78.1 23.8 %all_gather.31 = bf16[8,2048]{1,0:T(8,128)(2,1)S(1)} all-gather(bf16[8,256]{1,0:T(8,128)(2,1)S(1)} %pad_maximum_fusion.7), channel_id=1, replica_groups=mesh['dp'=2,'fsdp'=8] {'fsdp'}, dimensions={1}, use_global_device_ids=true | all-gather | bytes 36864 | tf_op jit(solution)/shard_map/all_gather | solution.py:78
  103.2 20.6 %collective-permute-done = bf16[512,2048]{1,0:T(8,128)(2,1)} collective-permute-done((bf16[512,2048]{1,0:T(8,128)(2,1)S(1)}, bf16[512,2048]{1,0:T(8,128)(2,1)}, u32[]{:S(2)}, u32[]{:S(2)}) %collective-permute-start) | collective-permute-done | bytes 2097184 | tf_op jit(solution)/shard_map/ppermute | solution.py:56
  123.8 16.4 %convolution_convert_fusion.5 = bf16[1024,3072]{1,0:T(8,128)(2,1)S(1)} fusion(bf16[2048,3072]{1,0:T(8,128)(2,1)} %all-gather.13.cloned.1.call-done, bf16[512,2048]{1,0:T(8,128)(2,1)} %collective-permute-done, bf16[512,2048]{1,0:T(8,128)(2,1)S(1)} %bitcast.165), kind=kOutput, calls=%fused_computation.51 | convolution fusion | flops 12896436224 | bytes 23068672 | tf_op jit(solution)/shard_map/dot_general | solution.py:28
  164.5 21.3 %collective-permute-done.2 = bf16[512,1024]{1,0:T(8,128)(2,1)} collective-permute-done((bf16[512,1024]{1,0:T(8,128)(2,1)S(1)}, bf16[512,1024]{1,0:T(8,128)(2,1)}, u32[]{:S(2)}, u32[]{:S(2)}) %collective-permute-start.2) | collective-permute-done | bytes 1048608 | tf_op jit(solution)/shard_map/ppermute | solution.py:56
  185.8 8.7 %fusion.40 = (f32[512]{0:T(512)S(1)}, bf16[512,2048]{1,0:T(8,128)(2,1)S(1)}) fusion(bf16[1,2048,2048]{2,1,0:T(8,128)(2,1)} %all-gather.25.cloned.1.call-done, bf16[512,1024]{1,0:T(8,128)(2,1)} %collective-permute-done.2, bf16[512,1024]{1,0:T(8,128)(2,1)S(1)} %bitcast.170, pred[]{:T(512)S(6)} %eq.4), kind=kOutput, calls=%fused_computation.74 | convolution fusion | flops 4308598272 | bytes 12584961 | tf_op jit(solution)/shard_map/dot_general | solution.py:28
  198.6 42.9 %collective-permute-done.3 = bf16[512,2048]{1,0:T(8,128)(2,1)} collective-permute-done((bf16[512,2048]{1,0:T(8,128)(2,1)S(1)}, bf16[512,2048]{1,0:T(8,128)(2,1)}, u32[]{:S(2)}, u32[]{:S(2)}) %collective-permute-start.3) | collective-permute-done | bytes 2097184 | tf_op jit(solution)/shard_map/ppermute | solution.py:56
  241.5 41.8 %all-gather.15.cloned.1.call-done = bf16[2048,8192]{1,0:T(8,128)(2,1)} async-done(((bf16[256,8192]{1,0:T(8,128)(2,1)}), bf16[2048,8192]{1,0:T(8,128)(2,1)}) %all-gather.15.cloned.1.call-update) | async-done | bytes 33554448 | tf_op jit(solution)/shard_map/all_gather | solution.py:59
  283.3 26.1 %convolution_convert_fusion.2 = bf16[512,8192]{1,0:T(8,128)(2,1)} fusion(bf16[512,2048]{1,0:T(8,128)(2,1)} %collective-permute-done.3, bf16[2048,8192]{1,0:T(8,128)(2,1)} %all-gather.15.cloned.1.call-done), kind=kOutput, calls=%fused_computation.8 | convolution fusion | flops 17184063488 | bytes 44040192 | tf_op jit(solution)/shard_map/dot_general | solution.py:28
  309.5 57.3 %all-gather.27.cloned.1.call-done = bf16[1,4096,2048]{2,1,0:T(8,128)(2,1)} async-done(((bf16[1,512,2048]{2,1,0:T(8,128)(2,1)}), bf16[1,4096,2048]{2,1,0:T(8,128)(2,1)}) %all-gather.27.cloned.1.call-update) | async-done | bytes 16777232 | tf_op jit(solution)/shard_map/all_gather | solution.py:59
  366.8 17.6 %fusion.2 = f32[512,2048]{1,0:T(8,128)} fusion(bf16[1,4096,2048]{2,1,0:T(8,128)(2,1)} %all-gather.27.cloned.1.call-done, bf16[512,8192]{1,0:T(8,128)(2,1)} %convolution_convert_fusion.2), kind=kOutput, calls=%fused_computation.2 | convolution fusion | flops 8606711808 | bytes 29360128 | tf_op jit(solution)/shard_map/dot_general | solution.py:28
  385.9 25.6 %convolution_convert_fusion.3 = bf16[512,8192]{1,0:T(8,128)(2,1)} fusion(bf16[512,2048]{1,0:T(8,128)(2,1)S(1)} %fusion.43, bf16[2048,8192]{1,0:T(8,128)(2,1)} %all-gather.15.cloned.1.call-done), kind=kOutput, calls=%fused_computation.9 | convolution fusion | flops 17184063488 | bytes 44040192 | tf_op jit(solution)/shard_map/dot_general | solution.py:28
  411.4 65.6 %collective-permute-done.4 = f32[512,2048]{1,0:T(8,128)} collective-permute-done((f32[512,2048]{1,0:T(8,128)}, f32[512,2048]{1,0:T(8,128)}, u32[]{:S(2)}, u32[]{:S(2)}) %collective-permute-start.4) | collective-permute-done | bytes 4194336 | tf_op jit(solution)/shard_map/ppermute | solution.py:56
  477.1 18.3 %fusion.44 = (f32[512]{0:T(512)S(1)}, bf16[512,2048]{1,0:T(8,128)(2,1)S(1)}) fusion(f32[512,2048]{1,0:T(8,128)} %collective-permute-done.4, bf16[1,4096,2048]{2,1,0:T(8,128)(2,1)} %all-gather.27.cloned.1.call-done, bf16[512,8192]{1,0:T(8,128)(2,1)} %convolution_convert_fusion.3), kind=kOutput, calls=%fused_computation.78 | convolution fusion | flops 8611954688 | bytes 31459328 | tf_op jit(solution)/shard_map/dot_general | solution.py:28
  498.3 45.4 %collective-permute-done.5 = bf16[512,2048]{1,0:T(8,128)(2,1)} collective-permute-done((bf16[512,2048]{1,0:T(8,128)(2,1)S(1)}, bf16[512,2048]{1,0:T(8,128)(2,1)}, u32[]{:S(2)}, u32[]{:S(2)}) %collective-permute-start.5) | collective-permute-done | bytes 2097184 | tf_op jit(solution)/shard_map/ppermute | solution.py:56
  543.7 16.8 %convolution_convert_fusion.4 = bf16[1024,3072]{1,0:T(8,128)(2,1)S(1)} fusion(bf16[2048,3072]{1,0:T(8,128)(2,1)} %all-gather.17.cloned.1.call-done, bf16[512,2048]{1,0:T(8,128)(2,1)} %collective-permute-done.5, bf16[512,2048]{1,0:T(8,128)(2,1)S(1)} %fusion.47), kind=kOutput, calls=%fused_computation.50 | convolution fusion | flops 12896436224 | bytes 23068672 | tf_op jit(solution)/shard_map/dot_general | solution.py:28
  584.4 21.0 %collective-permute-done.7 = bf16[512,1024]{1,0:T(8,128)(2,1)} collective-permute-done((bf16[512,1024]{1,0:T(8,128)(2,1)S(1)}, bf16[512,1024]{1,0:T(8,128)(2,1)}, u32[]{:S(2)}, u32[]{:S(2)}) %collective-permute-start.7) | collective-permute-done | bytes 1048608 | tf_op jit(solution)/shard_map/ppermute | solution.py:56
  605.4 8.7 %fusion.54 = (f32[512]{0:T(512)S(1)}, bf16[512,2048]{1,0:T(8,128)(2,1)S(1)}) fusion(bf16[1,2048,2048]{2,1,0:T(8,128)(2,1)} %all-gather.29.cloned.1.call-done, bf16[512,1024]{1,0:T(8,128)(2,1)} %collective-permute-done.7, bf16[512,1024]{1,0:T(8,128)(2,1)S(1)} %bitcast.169, pred[]{:T(512)S(6)} %eq.4), kind=kOutput, calls=%fused_computation.88 | convolution fusion | flops 4308598272 | bytes 12584961 | tf_op jit(solution)/shard_map/dot_general | solution.py:28
  616.4 17.4 %all-gather.19.cloned.1.call-done = bf16[2048,8192]{1,0:T(8,128)(2,1)} async-done(((bf16[256,8192]{1,0:T(8,128)(2,1)}), bf16[2048,8192]{1,0:T(8,128)(2,1)}) %all-gather.19.cloned.1.call-update) | async-done | bytes 33554448 | tf_op jit(solution)/shard_map/all_gather | solution.py:59
  633.9 26.8 %collective-permute-done.8 = bf16[512,2048]{1,0:T(8,128)(2,1)} collective-permute-done((bf16[512,2048]{1,0:T(8,128)(2,1)S(1)}, bf16[512,2048]{1,0:T(8,128)(2,1)}, u32[]{:S(2)}, u32[]{:S(2)}) %collective-permute-start.8) | collective-permute-done | bytes 2097184 | tf_op jit(solution)/shard_map/ppermute | solution.py:56
  660.6 26.2 %convolution_convert_fusion = bf16[512,8192]{1,0:T(8,128)(2,1)} fusion(bf16[512,2048]{1,0:T(8,128)(2,1)} %collective-permute-done.8, bf16[2048,8192]{1,0:T(8,128)(2,1)} %all-gather.19.cloned.1.call-done), kind=kOutput, calls=%fused_computation.6 | convolution fusion | flops 17184063488 | bytes 44040192 | tf_op jit(solution)/shard_map/dot_general | solution.py:28
  686.9 6.3 fusion.26
  693.2 10.5 %fusion.167 = f32[512,1024]{1,0:T(8,128)} fusion(bf16[512,4096]{1,0:T(8,128)(2,1)} %fusion.26, bf16[4096,1024]{1,0:T(8,128)(2,1)} %all-gather.21.cloned.1.call-done), kind=kOutput, calls=%fused_computation.241 | convolution fusion | flops 4294967296 | bytes 14680064 | tf_op jit(solution)/shard_map/dot_general | solution.py:28
  704.2 25.8 %convolution_convert_fusion.1 = bf16[512,8192]{1,0:T(8,128)(2,1)} fusion(bf16[512,2048]{1,0:T(8,128)(2,1)S(1)} %fusion.57, bf16[2048,8192]{1,0:T(8,128)(2,1)} %all-gather.19.cloned.1.call-done), kind=kOutput, calls=%fused_computation.7 | convolution fusion | flops 17184063488 | bytes 44040192 | tf_op jit(solution)/shard_map/dot_general | solution.py:28
  730.1 8.5 %fusion.168 = f32[512,1024]{1,0:T(8,128)S(1)} fusion(bf16[512,4096]{1,0:T(8,128)(2,1)} %fusion.26, bf16[4096,1024]{1,0:T(8,128)(2,1)} %all-gather.23.cloned.1.call-done), kind=kOutput, calls=%fused_computation.242 | convolution fusion | flops 4294967296 | bytes 14680064 | tf_op jit(solution)/shard_map/dot_general | solution.py:28
  740.0 12.1 %collective-permute-done.9 = f32[512,1024]{1,0:T(8,128)} collective-permute-done((f32[512,1024]{1,0:T(8,128)}, f32[512,1024]{1,0:T(8,128)}, u32[]{:S(2)}, u32[]{:S(2)}) %collective-permute-start.9) | collective-permute-done | bytes 2097184 | tf_op jit(solution)/shard_map/ppermute | solution.py:56
  752.1 9.3 %add_convert_fusion.6 = bf16[512,1024]{1,0:T(8,128)(2,1)S(1)} fusion(f32[512,1024]{1,0:T(8,128)} %collective-permute-done.9, bf16[4096,1024]{1,0:T(8,128)(2,1)S(1)} %copy-done.28, bf16[512,8192]{1,0:T(8,128)(2,1)} %convolution_convert_fusion.1), kind=kOutput, calls=%fused_computation.161 | convolution fusion | flops 4312793088 | bytes 19922944 | tf_op jit(solution)/shard_map/dot_general | solution.py:28
  761.5 31.6 %collective-permute-done.10 = f32[512,1024]{1,0:T(8,128)S(1)} collective-permute-done((f32[512,1024]{1,0:T(8,128)S(1)}, f32[512,1024]{1,0:T(8,128)S(1)}, u32[]{:S(2)}, u32[]{:S(2)}) %collective-permute-start.10) | collective-permute-done | bytes 2097184 | tf_op jit(solution)/shard_map/ppermute | solution.py:56
  793.1 8.8 %add_convert_fusion.5 = bf16[512,1024]{1,0:T(8,128)(2,1)S(1)} fusion(f32[512,1024]{1,0:T(8,128)S(1)} %collective-permute-done.10, bf16[4096,1024]{1,0:T(8,128)(2,1)S(1)} %bitcast.193, bf16[512,8192]{1,0:T(8,128)(2,1)} %convolution_convert_fusion.1), kind=kOutput, calls=%fused_computation.160 | convolution fusion | flops 4312793088 | bytes 19922944 | tf_op jit(solution)/shard_map/dot_general | solution.py:28
  (182 shorter events, 111.1 us)
Async XLA Ops:
  6.5 117.2 %all-gather.13.cloned.1.call-start = ((), (), s32[]{:S(2)}) async-start(), calls=%async_computation | async-start | bytes 14155776 | tf_op jit(solution)/shard_map/all_gather | solution.py:59
  14.9 149.6 %all-gather.25.cloned.1.call-start = ((), (), s32[]{:S(2)}) async-start(), calls=%async_computation.6 | async-start | bytes 9437184 | tf_op jit(solution)/shard_map/all_gather | solution.py:59
  18.1 265.2 %all-gather.15.cloned.1.call-start = ((), (), s32[]{:S(2)}) async-start(), calls=%async_computation.1 | async-start | bytes 37748736 | tf_op jit(solution)/shard_map/all_gather | solution.py:59
  48.3 318.5 %all-gather.27.cloned.1.call-start = ((), (), s32[]{:S(2)}) async-start(), calls=%async_computation.7 | async-start | bytes 18874368 | tf_op jit(solution)/shard_map/all_gather | solution.py:59
  55.4 442.9 %all-gather.17.cloned.1.call-start = ((), (), s32[]{:S(2)}) async-start(), calls=%async_computation.2 | async-start | bytes 14155776 | tf_op jit(solution)/shard_map/all_gather | solution.py:59
  57.1 527.3 %all-gather.29.cloned.1.call-start = ((), (), s32[]{:S(2)}) async-start(), calls=%async_computation.8 | async-start | bytes 9437184 | tf_op jit(solution)/shard_map/all_gather | solution.py:59
  57.7 576.2 %all-gather.19.cloned.1.call-start = ((), (), s32[]{:S(2)}) async-start(), calls=%async_computation.3 | async-start | bytes 37748736 | tf_op jit(solution)/shard_map/all_gather | solution.py:59
  73.7 619.4 %all-gather.21.cloned.1.call-start = ((), (), s32[]{:S(2)}) async-start(), calls=%async_computation.4 | async-start | bytes 9437184 | tf_op jit(solution)/shard_map/all_gather | solution.py:59
  75.2 48.5 %collective-permute-start = (bf16[512,2048]{1,0:T(8,128)(2,1)S(1)}, bf16[512,2048]{1,0:T(8,128)(2,1)}, u32[]{:S(2)}, u32[]{:S(2)}) collective-permute-start(bf16[512,2048]{1,0:T(8,128)(2,1)S(1)} %bitcast.164), channel_id=1, source_target_pairs={{0,8},{8,0},{1,9},{9,1},{2,10},{10,2},{3,11},{11,3},{4,12},{12,4},... | collective-permute-start | bytes 6291464 | tf_op jit(solution)/shard_map/ppermute | solution.py:56
  102.6 54.5 %copy-start.17 = (pred[256,256]{0,1:T(8,128)(4,1)}, pred[256,256]{0,1:T(8,128)(4,1)S(1)}, u32[]{:S(2)}) copy-start(pred[256,256]{0,1:T(8,128)(4,1)S(1)} %iota_compare_fusion) | copy-start | bytes 196612
  103.1 47.8 %copy-start.13 = (f32[256,64]{1,0:T(8,128)}, f32[256,64]{1,0:T(8,128)S(1)}, u32[]{:S(2)}) copy-start(f32[256,64]{1,0:T(8,128)S(1)} %get-tuple-element.69) | copy-start | bytes 196612
  103.1 47.8 %copy-start.15 = (f32[256,64]{1,0:T(8,128)}, f32[256,64]{1,0:T(8,128)S(1)}, u32[]{:S(2)}) copy-start(f32[256,64]{1,0:T(8,128)S(1)} %get-tuple-element.70) | copy-start | bytes 196612
  141.1 3.9 collective-permute-start.1
  161.8 24.0 %collective-permute-start.2 = (bf16[512,1024]{1,0:T(8,128)(2,1)S(1)}, bf16[512,1024]{1,0:T(8,128)(2,1)}, u32[]{:S(2)}, u32[]{:S(2)}) collective-permute-start(bf16[512,1024]{1,0:T(8,128)(2,1)S(1)} %bitcast.168), channel_id=1, source_target_pairs={{0,8},{8,0},{1,9},{9,1},{2,10},{10,2},{3,11},{11,3},{4,12},{12,4},... | collective-permute-start | bytes 3145736 | tf_op jit(solution)/shard_map/ppermute | solution.py:56
  185.8 8.8 %copy-start.8 = (bf16[2,256,2048]{2,1,0:T(8,128)(2,1)S(1)}, bf16[2,256,2048]{2,1,0:T(8,128)(2,1)}, u32[]{:S(2)}) copy-start(bf16[2,256,2048]{2,1,0:T(8,128)(2,1)} %param.12) | copy-start | bytes 6291460
  195.8 190.1 %copy-start.4 = (bf16[512,2048]{1,0:T(8,128)(2,1)}, bf16[512,2048]{1,0:T(8,128)(2,1)S(1)}, u32[]{:S(2)}) copy-start(bf16[512,2048]{1,0:T(8,128)(2,1)S(1)} %fusion.43) | copy-start | bytes 6291460
  195.8 45.7 %collective-permute-start.3 = (bf16[512,2048]{1,0:T(8,128)(2,1)S(1)}, bf16[512,2048]{1,0:T(8,128)(2,1)}, u32[]{:S(2)}, u32[]{:S(2)}) collective-permute-start(bf16[512,2048]{1,0:T(8,128)(2,1)S(1)} %fusion.43), channel_id=1, source_target_pairs={{0,8},{8,0},{1,9},{9,1},{2,10},{10,2},{3,11},{11,3},{4,12},{12,4},... | collective-permute-start | bytes 6291464 | tf_op jit(solution)/shard_map/ppermute | solution.py:56
  198.6 531.5 %all-gather.23.cloned.1.call-start = ((), (), s32[]{:S(2)}) async-start(), calls=%async_computation.5 | async-start | bytes 9437184 | tf_op jit(solution)/shard_map/all_gather | solution.py:59
  384.4 92.7 %collective-permute-start.4 = (f32[512,2048]{1,0:T(8,128)}, f32[512,2048]{1,0:T(8,128)}, u32[]{:S(2)}, u32[]{:S(2)}) collective-permute-start(f32[512,2048]{1,0:T(8,128)} %fusion.2), channel_id=1, source_target_pairs={{0,8},{8,0},{1,9},{9,1},{2,10},{10,2},{3,11},{11,3},{4,12},{12,4},... | collective-permute-start | bytes 12582920 | tf_op jit(solution)/shard_map/ppermute | solution.py:56
  411.4 84.0 %copy-start.5 = (bf16[512,2048]{1,0:T(8,128)(2,1)S(1)}, bf16[512,2048]{1,0:T(8,128)(2,1)}, u32[]{:S(2)}) copy-start(bf16[512,2048]{1,0:T(8,128)(2,1)} %copy-done.4) | copy-start | bytes 6291460
  411.4 84.0 %copy-start.21 = (f32[1,2048]{1,0:T(1,128)S(1)}, f32[1,2048]{1,0:T(1,128)}, u32[]{:S(2)}) copy-start(f32[1,2048]{1,0:T(1,128)} %get-tuple-element.56) | copy-start | bytes 24580
  496.6 63.9 %copy-start.2 = (bf16[512,2048]{1,0:T(8,128)(2,1)}, bf16[512,2048]{1,0:T(8,128)(2,1)S(1)}, u32[]{:S(2)}) copy-start(bf16[512,2048]{1,0:T(8,128)(2,1)S(1)} %fusion.47) | copy-start | bytes 6291460
  496.6 47.1 %collective-permute-start.5 = (bf16[512,2048]{1,0:T(8,128)(2,1)S(1)}, bf16[512,2048]{1,0:T(8,128)(2,1)}, u32[]{:S(2)}, u32[]{:S(2)}) collective-permute-start(bf16[512,2048]{1,0:T(8,128)(2,1)S(1)} %fusion.47), channel_id=1, source_target_pairs={{0,8},{8,0},{1,9},{9,1},{2,10},{10,2},{3,11},{11,3},{4,12},{12,4},... | collective-permute-start | bytes 6291464 | tf_op jit(solution)/shard_map/ppermute | solution.py:56
  561.4 3.7 collective-permute-start.6
  581.8 23.6 %collective-permute-start.7 = (bf16[512,1024]{1,0:T(8,128)(2,1)S(1)}, bf16[512,1024]{1,0:T(8,128)(2,1)}, u32[]{:S(2)}, u32[]{:S(2)}) collective-permute-start(bf16[512,1024]{1,0:T(8,128)(2,1)S(1)} %bitcast.171), channel_id=1, source_target_pairs={{0,8},{8,0},{1,9},{9,1},{2,10},{10,2},{3,11},{11,3},{4,12},{12,4},... | collective-permute-start | bytes 3145736 | tf_op jit(solution)/shard_map/ppermute | solution.py:56
  615.3 45.3 %collective-permute-start.8 = (bf16[512,2048]{1,0:T(8,128)(2,1)S(1)}, bf16[512,2048]{1,0:T(8,128)(2,1)}, u32[]{:S(2)}, u32[]{:S(2)}) collective-permute-start(bf16[512,2048]{1,0:T(8,128)(2,1)S(1)} %fusion.57), channel_id=1, source_target_pairs={{0,8},{8,0},{1,9},{9,1},{2,10},{10,2},{3,11},{11,3},{4,12},{12,4},... | collective-permute-start | bytes 6291464 | tf_op jit(solution)/shard_map/ppermute | solution.py:56
  703.6 48.5 %collective-permute-start.9 = (f32[512,1024]{1,0:T(8,128)}, f32[512,1024]{1,0:T(8,128)}, u32[]{:S(2)}, u32[]{:S(2)}) collective-permute-start(f32[512,1024]{1,0:T(8,128)} %fusion.167), channel_id=1, source_target_pairs={{0,8},{8,0},{1,9},{9,1},{2,10},{10,2},{3,11},{11,3},{4,12},{12,4},... | collective-permute-start | bytes 6291464 | tf_op jit(solution)/shard_map/ppermute | solution.py:56
  730.1 22.1 %copy-start.28 = (bf16[4096,1024]{1,0:T(8,128)(2,1)S(1)}, bf16[4096,1024]{1,0:T(8,128)(2,1)}, u32[]{:S(2)}) copy-start(bf16[4096,1024]{1,0:T(8,128)(2,1)} %all-gather.21.cloned.1.call-done) | copy-start | bytes 25165828
  730.1 63.0 %slice-start = ((s8[8388608]{0:T(1024)(128)(4,1)}), s8[4194304]{0:T(1024)(128)(4,1)S(1)}, s32[]{:S(2)}) async-start(s8[8388608]{0:T(1024)(128)(4,1)} %bitcast.192), calls=%async_computation.9 | async-start | bytes 8388608
  738.5 54.5 %slice-start.1 = ((s8[8388608]{0:T(1024)(128)(4,1)}), s8[4194304]{0:T(1024)(128)(4,1)S(1)}, s32[]{:S(2)}) async-start(s8[8388608]{0:T(1024)(128)(4,1)} %bitcast.192), calls=%async_computation.10 | async-start | bytes 8388608
  738.5 54.5 %collective-permute-start.10 = (f32[512,1024]{1,0:T(8,128)S(1)}, f32[512,1024]{1,0:T(8,128)S(1)}, u32[]{:S(2)}, u32[]{:S(2)}) collective-permute-start(f32[512,1024]{1,0:T(8,128)S(1)} %fusion.168), channel_id=1, source_target_pairs={{0,8},{8,0},{1,9},{9,1},{2,10},{10,2},{3,11},{11,3},{4,12},{12,4},... | collective-permute-start | bytes 6291464 | tf_op jit(solution)/shard_map/ppermute | solution.py:56
  761.5 40.9 %copy-start.19 = (f32[1,2048]{1,0:T(1,128)S(1)}, f32[1,2048]{1,0:T(1,128)}, u32[]{:S(2)}) copy-start(f32[1,2048]{1,0:T(1,128)} %get-tuple-element.53) | copy-start | bytes 24580
  (19 other events, 69.0 us)
Sparse Core Ops, SparseCore 0:
  15.0 66.0 all-gather.12
  82.7 46.0 all-gather.24
  130.5 152.8 all-gather.14
  284.8 81.9 all-gather.26
  368.2 63.7 all-gather.16
  433.5 45.7 all-gather.28
  480.9 152.8 all-gather.18
  635.5 46.3 all-gather.20
  683.5 45.6 all-gather.22

commit v2 on v0

v2 whole, which is shorter than its diff:
```python
import functools

import jax
import jax.numpy as jnp
import numpy as np
from jax import lax
from jax.experimental import pallas as pl
from jax.experimental.pallas import tpu as pltpu
from jax.sharding import PartitionSpec as P

HEAD_DIM = 128
EPS = 1e-6
THETA = 500000.0
SLAB = 1024
AHEAD = 2
LAG = 2
F32 = jnp.float32
BF16 = jnp.bfloat16


def rope_tables(seq_len):
    positions = np.arange(seq_len, dtype=np.float32)
    inv_freq = np.power(np.float32(THETA), -2.0 * np.arange(HEAD_DIM // 2, dtype=np.float32) / np.float32(HEAD_DIM)).astype(np.float32)
    angles = positions[:, None] * inv_freq[None, :]
    cos, sin = np.cos(angles), np.sin(angles)
    return np.concatenate([cos, cos], axis=1), np.concatenate([-sin, sin], axis=1)


def dot(left, right):
    return jnp.dot(left, right, preferred_element_type=F32)


def kernel(dims, tokens, gains, cos_ref, sin_ref, wq, wk, wv, wo, wg, wu, wd, out, gat,
           x2, qkv, att, att_in, alin, h2, mid, p_own, p_out, p_in, wbuf, stat, stat_in, gvec,
           sem_a, sem_b, sem_c, sem_s, sem_w, sem_g, sem_y, sem_p, sem_l):
    n, n_layers, n_tok, seq_len, width, rows, ff_blk, d_rows = dims
    half = width // 2
    n_heads = half // HEAD_DIM
    n_qkv, n_out, n_gu, n_down = 3, width // SLAB, n, width // 512
    per_layer = n_qkv + n_out + n_gu + n_down
    n_stage = per_layer * n_layers
    first_out, first_gu, first_down = n_qkv, n_qkv + n_out, n_qkv + n_out + n_gu
    me = lax.axis_index('fsdp')
    group = lax.axis_index('dp')
    part = lax.rem(group, 2)
    pair = {'dp': group + 1 - 2 * part}
    left = lax.rem(me + n - 2, n)
    right = lax.rem(me + 2, n)
    far = lax.rem(me + 4, n)
    sib = me + 1 - 2 * lax.rem(me, 2)
    own_rows = pl.ds(0, n_tok)
    pair_rows = pl.ds(n_tok, n_tok)

    def send(src, dst, s_sem, r_sem, dev):
        copy = pltpu.make_async_remote_copy(src_ref=src, dst_ref=dst, send_sem=s_sem, recv_sem=r_sem, device_id=dev,
                                            device_id_type=pl.DeviceIdType.MESH)
        copy.start()
        return copy

    def arrive(ref, sem):
        pltpu.make_async_copy(ref, ref, sem).wait()

    def own_blocks(layer, pos, do):
        for i, w in enumerate((wq, wk, wv)):
            @pl.when(pos == i)
            def _(w=w):
                do(w.at[layer, :, pl.ds(pl.multiple_of(part * half, 128), half)], slice(0, SLAB))

        @pl.when(jnp.logical_and(pos >= first_out, pos < first_gu))
        def _():
            do(wo.at[layer, :, pl.ds(pl.multiple_of((pos - first_out) * SLAB, 128), SLAB)], slice(0, SLAB))

        @pl.when(jnp.logical_and(pos >= first_gu, pos < first_down))
        def _():
            cols = pl.ds(pl.multiple_of((pos - first_gu) * 2 * ff_blk + part * ff_blk, 128), ff_blk)
            do(wg.at[layer, :, cols], slice(0, ff_blk))
            do(wu.at[layer, :, cols], slice(ff_blk, 2 * ff_blk))

        @pl.when(pos >= first_down)
        def _():
            cols = pl.ds(pl.multiple_of((pos - first_down) * 512, 128), 512)
            for k in range(2):
                do(wd.at[layer, pl.ds(pl.multiple_of(part * d_rows + k * rows, 128), rows), cols], slice(k * 512, (k + 1) * 512))

    def start_own(s):
        def do(src, cols):
            dst = gat.at[s, me, :, cols]
            send(src, dst, sem_s.at[s], sem_a.at[s], {'fsdp': right})
            send(src, dst, sem_s.at[s], sem_a.at[s], {'fsdp': left})
            send(src, dst, sem_s.at[s], sem_c.at[s], {'fsdp': sib})
        own_blocks(s // per_layer, lax.rem(s, per_layer), do)

    def pump(s):
        @pl.when(s < n_stage)
        def _():
            arrive(gat.at[s, pl.ds(0, 2)], sem_a.at[s])
            top, bottom = pl.ds(0, rows // 2), pl.ds(rows // 2, rows // 2)
            block = gat.at[s, left, top]
            send(block, block, sem_s.at[s], sem_b.at[s], {'fsdp': right})
            block = gat.at[s, right, bottom]
            send(block, block, sem_s.at[s], sem_b.at[s], {'fsdp': left})
            for origin in (left, right):
                block = gat.at[s, origin]
                send(block, block, sem_s.at[s], sem_c.at[s], {'fsdp': sib})

        @pl.when(s + AHEAD < n_stage)
        def _():
            start_own(s + AHEAD)

        @pl.when(jnp.logical_and(s >= LAG, s < n_stage + LAG))
        def _():
            t = s - LAG
            block = gat.at[t, far]
            arrive(block, sem_b.at[t])
            send(block, block, sem_s.at[t], sem_c.at[t], {'fsdp': sib})

    def stage_ready(s):
        arrive(gat.at[s, pl.ds(0, 4)], sem_c.at[s])

    def load(layer, pos, slot):
        s = layer * per_layer + pos
        for k in range(1, n):
            d = lax.rem(me + k, n)
            pltpu.make_async_copy(gat.at[s, d], wbuf.at[slot, d], sem_w.at[slot]).start()
        own_blocks(layer, pos, lambda src, cols: pltpu.make_async_copy(src, wbuf.at[slot, me, :, cols], sem_w.at[slot]).start())

    def loaded(slot):
        arrive(wbuf.at[slot], sem_w.at[slot])

    def tiles(layer, first, count, repeat, compute, pumps):
        stage, fresh = repeat

        def fetch(it):
            pos = first + stage(it)

            @pl.when(fresh(it))
            def _():
                stage_ready(layer * per_layer + pos)
            load(layer, pos, lax.rem(it, 2))

        pumps(jnp.int32(0))
        fetch(jnp.int32(0))

        def body(it, carry):
            @pl.when(it + 1 < count)
            def _():
                pumps(it + 1)
                fetch(it + 1)
            slot = lax.rem(it, 2)
            loaded(slot)
            compute(it, slot)
            return carry
        lax.fori_loop(0, count, body, 0)

    def weight(slot, cols):
        return wbuf[slot, :, :, cols].reshape(n * rows, cols.stop - cols.start)

    barrier = pltpu.get_barrier_semaphore()
    for k in range(1, n):
        pl.semaphore_signal(barrier, inc=1, device_id={'fsdp': lax.rem(me + k, n)}, device_id_type=pl.DeviceIdType.MESH)
    pl.semaphore_signal(barrier, inc=1, device_id=pair, device_id_type=pl.DeviceIdType.MESH)
    pl.semaphore_wait(barrier, n)

    for s in range(AHEAD):
        start_own(jnp.int32(s))
    x_copy = send(tokens, x2.at[pair_rows], sem_y.at[0], sem_y.at[1], pair)
    my_gain = gvec.at[:, pl.ds(pl.multiple_of(me * rows, 128), rows)]
    gain_copies = [send(gains, my_gain, sem_g.at[0], sem_g.at[1], {'fsdp': lax.rem(me + k, n)}) for k in range(1, n)]
    local = [pltpu.make_async_copy(tokens, x2.at[own_rows], sem_l.at[0]), pltpu.make_async_copy(gains, my_gain, sem_l.at[1])]
    for c in local:
        c.start()
    for c in local:
        c.wait()
    gain_ref = gvec.at[:, pl.ds(0, (n - 1) * rows)]
    arrive(gain_ref, sem_g.at[0])
    arrive(gain_ref, sem_g.at[1])
    x_copy.wait_send()
    for s in range(3):
        pump(jnp.int32(s))

    blk = 64

    def pick_gain(row, cols):
        table = gvec[:, cols]
        chosen = lax.broadcasted_iota(jnp.int32, table.shape, 0) == row
        return jnp.sum(jnp.where(chosen, table, 0.0), axis=0, keepdims=True)

    def residual_norm(res, lin, dst, gain_row):
        gain = pick_gain(gain_row, slice(None))

        def body(i, carry):
            r = pl.ds(pl.multiple_of(i * blk, blk), blk)
            v = lin(r)
            inv = lax.rsqrt(jnp.mean(v * v, axis=-1, keepdims=True) + EPS)
            dst[r, :] = (res[r, :].astype(F32) + v * inv * gain).astype(BF16)
            return carry
        lax.fori_loop(0, n_tok // blk, body, 0)

    def layer_body(layer, carry):
        base = layer * per_layer

        def qkv_compute(it, slot):
            @pl.when(it == n_qkv)
            def _():
                arrive(x2.at[pair_rows], sem_y.at[1])
            kind = lax.rem(it, n_qkv)
            r = pl.ds(pl.multiple_of((it // n_qkv) * n_tok, n_tok), n_tok)
            for k in range(SLAB // 512):
                val = dot(x2[r, :], weight(slot, slice(k * 512, (k + 1) * 512))).astype(BF16)
                qkv[r, pl.ds(pl.multiple_of(kind * half + k * 512, 128), 512)] = val
                sq = val.astype(F32)
                ssq = jnp.sum(sq * sq, axis=-1, keepdims=True)
                if k == 0:
                    total = ssq
                else:
                    total = total + ssq
            lane = lax.broadcasted_iota(jnp.int32, (n_tok, 128), 1)
            spread = jnp.broadcast_to(total, (n_tok, 128))

            @pl.when(kind == 0)
            def _():
                stat[r, :] = spread

            @pl.when(kind == 1)
            def _():
                stat[r, :] = jnp.where(lane < 64, stat[r, :], spread)

        def qkv_pumps(it):
            @pl.when(it < n_qkv)
            def _():
                pump(base + 3 + it)
        tiles(layer, 0, 2 * n_qkv, (lambda it: lax.rem(it, n_qkv), lambda it: it < n_qkv), qkv_compute, qkv_pumps)

        copies = [send(stat.at[own_rows], stat_in.at[pair_rows], sem_y.at[2], sem_y.at[3], pair),
                  send(stat.at[pair_rows], stat_in.at[own_rows], sem_y.at[4], sem_y.at[5], pair)]
        pump(base + 6)
        for c in copies:
            c.wait()

        n_seq = n_tok // seq_len

        def attend(it, carry):
            seq = lax.rem(it + n_seq, 2 * n_seq)
            r = pl.ds(pl.multiple_of(seq * seq_len, seq_len), seq_len)
            sums = (stat[r, :] + stat_in[r, :]) * (1.0 / width)
            inv = lax.rsqrt(sums + EPS)
            inv_q, inv_k = inv[:, 0:1], inv[:, 64:65]
            causal = lax.broadcasted_iota(jnp.int32, (seq_len, seq_len), 0) >= lax.broadcasted_iota(jnp.int32, (seq_len, seq_len), 1)

            def norm_rope(vals, inv_rms, gain):
                v = vals.astype(F32) * inv_rms * gain
                return (v * cos_ref[...] + pltpu.roll(v, HEAD_DIM // 2, 1) * sin_ref[...]).astype(BF16)

            def head(h, c2):
                col = pl.multiple_of(h * HEAD_DIM, HEAD_DIM)
                gcol = pl.ds(pl.multiple_of(part * half + col, HEAD_DIM), HEAD_DIM)
                q = norm_rope(qkv[r, pl.ds(col, HEAD_DIM)], inv_q, pick_gain(layer, gcol))
                k = norm_rope(qkv[r, pl.ds(pl.multiple_of(half + col, HEAD_DIM), HEAD_DIM)], inv_k, pick_gain(n_layers + layer, gcol))
                v = qkv[r, pl.ds(pl.multiple_of(2 * half + col, HEAD_DIM), HEAD_DIM)]
                sc = lax.dot_general(q, k, (((1,), (1,)), ((), ())), preferred_element_type=F32) * HEAD_DIM ** -0.5
                sc = jnp.where(causal, sc, -jnp.inf)
                e = jnp.exp(sc - jnp.max(sc, axis=-1, keepdims=True))
                p = (e / jnp.sum(e, axis=-1, keepdims=True)).astype(BF16)
                att[r, pl.ds(col, HEAD_DIM)] = dot(p, v).astype(BF16)
                return c2
            lax.fori_loop(0, n_heads, head, 0)

            @pl.when(it < 3)
            def _():
                pump(base + 7 + it)

            @pl.when(it == n_seq - 1)
            def _():
                send(att.at[pair_rows], att_in, sem_y.at[6], sem_y.at[7], pair)
            return carry
        lax.fori_loop(0, 2 * n_seq, attend, 0)
        arrive(att_in, sem_y.at[6])
        arrive(att_in, sem_y.at[7])

        def out_compute(it, slot):
            q = n // 2
            for k in range(SLAB // 512):
                cols = slice(k * 512, (k + 1) * 512)
                w_mine = wbuf[slot, pl.ds(part * q, q), :, cols].reshape(q * rows, 512)
                w_theirs = wbuf[slot, pl.ds((1 - part) * q, q), :, cols].reshape(q * rows, 512)
                val = dot(att[own_rows, :], w_mine) + dot(att_in[...], w_theirs)
                alin[:, pl.ds(pl.multiple_of(it * SLAB + k * 512, 128), 512)] = val.astype(BF16)

        def out_pumps(it):
            @pl.when(it == 0)
            def _():
                pump(base + 10)
        tiles(layer, first_out, n_out, (lambda it: it, lambda it: it >= 0), out_compute, out_pumps)
        residual_norm(x2, lambda r: alin[r, :].astype(F32), h2, 2 * n_layers + layer)
        h_copy = send(h2.at[own_rows], h2.at[pair_rows], sem_y.at[8], sem_y.at[9], pair)

        def gu_compute(it, slot):
            @pl.when(it == n_gu)
            def _():
                h_copy.wait()
            d = lax.rem(it, n_gu)
            r = pl.ds(pl.multiple_of((it // n_gu) * n_tok, n_tok), n_tok)
            for k in range(2):
                w = ff_blk // 2
                g = dot(h2[r, :], weight(slot, slice(k * w, (k + 1) * w))).astype(BF16).astype(F32)
                u = dot(h2[r, :], weight(slot, slice(ff_blk + k * w, ff_blk + (k + 1) * w))).astype(BF16).astype(F32)
                mid[r, pl.ds(pl.multiple_of(k * n * rows + d * w, 128), w)] = (jax.nn.silu(g) * u).astype(BF16)

        def gu_pumps(it):
            @pl.when(jnp.logical_and(it >= 3, it < n_gu))
            def _():
                pump(base + 8 + it)

            @pl.when(jnp.logical_or(it == 11, it == 14))
            def _():
                pump(base + 16 + (it - 11) // 3)
        tiles(layer, first_gu, 2 * n_gu, (lambda it: lax.rem(it, n_gu), lambda it: it < n_gu), gu_compute, gu_pumps)

        def down_compute(it, slot):
            c = it // 2
            cols = pl.ds(pl.multiple_of(c * 512, 512), 512)
            mine = lax.rem(it, 2)
            r = pl.ds(pl.multiple_of((1 - mine) * n_tok, n_tok), n_tok)
            k_half = n * rows
            val = dot(mid[r, 0:k_half], weight(slot, slice(0, 512))) + dot(mid[r, k_half:2 * k_half], weight(slot, slice(512, 1024)))

            @pl.when(mine == 1)
            def _():
                p_own[:, cols] = val

            @pl.when(mine == 0)
            def _():
                p_out[:, cols] = val
                send(p_out.at[:, cols], p_in.at[:, cols], sem_p.at[0, c], sem_p.at[1, c], pair)

        def down_pumps(it):
            @pl.when(jnp.logical_or(it == 4, it == 6))
            def _():
                pump(base + 18 + (it - 4) // 2)
        tiles(layer, first_down, 2 * n_down, (lambda it: it // 2, lambda it: lax.rem(it, 2) == 0), down_compute, down_pumps)
        for c in range(n_down):
            for k in range(2):
                arrive(p_in.at[:, pl.ds(c * 512, 512)], sem_p.at[k, c])
        residual_norm(h2, lambda r: (p_own[r, :] + p_in[r, :]).astype(BF16).astype(F32), x2, 3 * n_layers + layer)

        @pl.when(layer + 1 < n_layers)
        def _():
            send(x2.at[own_rows], x2.at[pair_rows], sem_y.at[0], sem_y.at[1], pair).wait_send()
        return carry
    lax.fori_loop(0, n_layers, layer_body, 0)

    done = pltpu.make_async_copy(x2.at[own_rows], out, sem_l.at[0])
    done.start()
    done.wait()

    def drain(s, carry):
        arrive(gat.at[s, pl.ds(0, 7)], sem_s.at[s])
        return carry
    lax.fori_loop(0, n_stage, drain, 0)


def solution(mesh):
    n_fsdp = mesh.shape['fsdp']

    def local_fn(tokens, weights):
        w_query, w_key, w_value, w_out, w_gate, w_up, w_down, g_query, g_key, g_attn, g_mlp = weights
        n_layers, rows, width = w_query.shape
        n_seq, seq_len, _ = tokens.shape
        n_tok = n_seq * seq_len
        ff = w_gate.shape[2]
        half = width // 2
        ff_blk = ff // n_fsdp // 2
        d_rows = w_down.shape[1] // 2
        dims = (n_fsdp, n_layers, n_tok, seq_len, width, rows, ff_blk, d_rows)
        n_stage = n_layers * (3 + width // SLAB + n_fsdp + width // 512)
        gains = jnp.concatenate([g_query, g_key, g_attn, g_mlp], axis=0).astype(F32)
        cos_tab, sin_tab = rope_tables(seq_len)
        hbm = pl.BlockSpec(memory_space=pl.ANY)
        vmem = pl.BlockSpec(memory_space=pltpu.VMEM)
        result, _ = pl.pallas_call(
            functools.partial(kernel, dims),
            out_shape=(jax.ShapeDtypeStruct((n_tok, width), BF16), jax.ShapeDtypeStruct((n_stage, n_fsdp, rows, SLAB), BF16)),
            in_specs=[hbm, vmem, vmem, vmem] + [hbm] * 7,
            out_specs=(hbm, hbm),
            scratch_shapes=[
                pltpu.VMEM((2 * n_tok, width), BF16),
                pltpu.VMEM((2 * n_tok, 3 * half), BF16),
                pltpu.VMEM((2 * n_tok, half), BF16),
                pltpu.VMEM((n_tok, half), BF16),
                pltpu.VMEM((n_tok, width), BF16),
                pltpu.VMEM((2 * n_tok, width), BF16),
                pltpu.VMEM((2 * n_tok, ff // 2), BF16),
                pltpu.VMEM((n_tok, width), F32),
                pltpu.VMEM((n_tok, width), F32),
                pltpu.VMEM((n_tok, width), F32),
                pltpu.VMEM((2, n_fsdp, rows, SLAB), BF16),
                pltpu.VMEM((2 * n_tok, 128), F32),
                pltpu.VMEM((2 * n_tok, 128), F32),
                pltpu.VMEM((4 * n_layers, width), F32),
                pltpu.SemaphoreType.DMA((n_stage,)),
                pltpu.SemaphoreType.DMA((n_stage,)),
                pltpu.SemaphoreType.DMA((n_stage,)),
                pltpu.SemaphoreType.DMA((n_stage,)),
                pltpu.SemaphoreType.DMA((2,)),
                pltpu.SemaphoreType.DMA((2,)),
                pltpu.SemaphoreType.DMA((10,)),
                pltpu.SemaphoreType.DMA((2, width // 512)),
                pltpu.SemaphoreType.DMA((2,)),
            ],
            compiler_params=pltpu.CompilerParams(collective_id=0, has_side_effects=True, vmem_limit_bytes=62 * 1024 * 1024),
        )(tokens.reshape(n_tok, width), gains, jnp.asarray(cos_tab), jnp.asarray(sin_tab), w_query, w_key, w_value, w_out, w_gate, w_up, w_down)
        return result.reshape(n_seq, seq_len, width)

    mapped = jax.shard_map(local_fn, mesh=mesh, in_specs=(P(('dp', 'fsdp')), P(None, 'fsdp')), out_specs=P(('dp', 'fsdp')), check_vma=False)

    def run(tokens, w_query, w_key, w_value, w_out, w_gate, w_up, w_down, g_query, g_key, g_attn, g_mlp):
        return mapped(tokens, (w_query, w_key, w_value, w_out, w_gate, w_up, w_down, g_query, g_key, g_attn, g_mlp))

    return run
```

time: 1360 us -> 787 us (0.58)
  waiting for transfers between devices: 843 us -> 0 us
  Pallas kernels: 0 us -> 783 us
  matrix products: 228 us -> 0 us
  blocking collectives: 179 us -> 0 us
  local copies, waits for them, and re-layouts: 59.9 us -> 3.16 us
  other arithmetic: 28.4 us -> 1.34 us
  between operations: 14.4 us -> 0.01 us
    all_gather x14 -> x0, waiting for transfers between devices: 839 us -> none  [gather_rows(): return lax.all_gather(arr_w[layer_idx], 'fsdp', axis=0, tiled=True)]
    pallas_call x0 -> x1, Pallas kernels: none -> 783 us  [local_fn(): pl.pallas_call(functools.partial(kernel, dims), out_shape=(jax.ShapeDtype...]
    dot_general x18 -> x0, matrix products: 228 us -> none  [the longest x14 218 us: dot_bf16(): jnp.dot(left, right, preferred_element_type=jnp.float32)]
    all_gather x8 -> x0, blocking collectives: 179 us -> none  [gather_rows(): return lax.all_gather(arr_w[layer_idx], 'fsdp', axis=0, tiled=True)]
    slice x14 -> x0, local copies, waits for them, and re-layouts: 34.4 us -> none  [the longest x11 27.6 us: gather_rows(): return lax.all_gather(arr_w[layer_idx], 'fsdp', axis=0, tiled=True)]
    unnamed x64 -> x1, local copies, waits for them, and re-layouts: 18.6 us -> 3.16 us
  transfers between devices with their start and end apart: 14 -> 0, of which waited for: 10 -> 0; matrix products, arithmetic and copies ran while one was open for 21% -> 0% of each run, Pallas kernels for 0% -> 0%
where the time goes in v2:
time: 787 us
  Pallas kernels  783 us (99%)
    pallas_call x1, Pallas kernels, local_fn(): pl.pallas_call(functools.partial(kernel, dims), out_shape=(jax.ShapeDtype...  783 us

profile of v2, /device:TPU:112, one launch (start us, length us, event | category | flops | bytes accessed | tf_op | source)
XLA Modules:
  0.0 787.2 jit_solution(13776407883244235541)
XLA Ops:
  0.0 1.3 maximum_convert_fusion.gains
  1.3 782.7 %shard_map.136 = (bf16[512,2048]{1,0:T(8,128)(2,1)}, bf16[34,8,256,1024]{3,2,1,0:T(8,128)(2,1)}) custom-call(bf16[512,2048]{1,0:T(8,128)(2,1)} %bitcast.2, f32[8,256]{1,0:T(8,128)} %maximum_convert_fusion.gains, f32[256,128]{1,0:T(8,128)} %constant.4.clone.cos_ref, f32[256,128]{1,0:T(8,128)} %constant.5.clone.sin_ref, bf16[2,256,2048]{2,1,0:T(8,128)(2,1)} %wq.1, ...), custom_call_target="tpu_custom_call" | custom-call | tf_op jit(solution)/shard_map/pallas_call | solution.py:380
  784.1 3.2 copy.16

commit v3 on v2

--- a/solution.py
+++ b/solution.py
@@ -12,7 +12,7 @@
 EPS = 1e-6
 THETA = 500000.0
 SLAB = 1024
-AHEAD = 2
+AHEAD = 3
 LAG = 2
 F32 = jnp.float32
 BF16 = jnp.bfloat16
@@ -199,9 +199,18 @@
     def layer_body(layer, carry):
         base = layer * per_layer
 
+        def pump_span(lo, hi):
+            lo, hi = (jnp.where(layer == 0, *v) if isinstance(v, tuple) else v for v in (lo, hi))
+
+            def one(s, c):
+                pump(base + s)
+                return c
+            lax.fori_loop(lo, hi, one, 0)
+
         def qkv_compute(it, slot):
             @pl.when(it == n_qkv)
             def _():
+                pump_span(5, (5, 7))
                 arrive(x2.at[pair_rows], sem_y.at[1])
             kind = lax.rem(it, n_qkv)
             r = pl.ds(pl.multiple_of((it // n_qkv) * n_tok, n_tok), n_tok)
@@ -226,14 +235,18 @@
                 stat[r, :] = jnp.where(lane < 64, stat[r, :], spread)
 
         def qkv_pumps(it):
-            @pl.when(it < n_qkv)
-            def _():
-                pump(base + 3 + it)
+            @pl.when(it == 1)
+            def _():
+                pump_span((3, 4), 4)
+
+            @pl.when(it == 2)
+            def _():
+                pump_span(4, 5)
         tiles(layer, 0, 2 * n_qkv, (lambda it: lax.rem(it, n_qkv), lambda it: it < n_qkv), qkv_compute, qkv_pumps)
 
         copies = [send(stat.at[own_rows], stat_in.at[pair_rows], sem_y.at[2], sem_y.at[3], pair),
                   send(stat.at[pair_rows], stat_in.at[own_rows], sem_y.at[4], sem_y.at[5], pair)]
-        pump(base + 6)
+        pump_span((5, 7), (6, 8))
         for c in copies:
             c.wait()
 
@@ -265,13 +278,17 @@
                 return c2
             lax.fori_loop(0, n_heads, head, 0)
 
-            @pl.when(it < 3)
-            def _():
-                pump(base + 7 + it)
-
             @pl.when(it == n_seq - 1)
             def _():
                 send(att.at[pair_rows], att_in, sem_y.at[6], sem_y.at[7], pair)
+
+            @pl.when(it == 1)
+            def _():
+                pump_span((6, 8), (7, 9))
+
+            @pl.when(it == 3)
+            def _():
+                pump_span((7, 9), (7, 10))
             return carry
         lax.fori_loop(0, 2 * n_seq, attend, 0)
         arrive(att_in, sem_y.at[6])
@@ -287,12 +304,11 @@
                 alin[:, pl.ds(pl.multiple_of(it * SLAB + k * 512, 128), 512)] = val.astype(BF16)
 
         def out_pumps(it):
-            @pl.when(it == 0)
-            def _():
-                pump(base + 10)
+            return
         tiles(layer, first_out, n_out, (lambda it: it, lambda it: it >= 0), out_compute, out_pumps)
         residual_norm(x2, lambda r: alin[r, :].astype(F32), h2, 2 * n_layers + layer)
         h_copy = send(h2.at[own_rows], h2.at[pair_rows], sem_y.at[8], sem_y.at[9], pair)
+        pump_span((7, 10), (7, 11))
 
         def gu_compute(it, slot):
             @pl.when(it == n_gu)
@@ -307,13 +323,9 @@
                 mid[r, pl.ds(pl.multiple_of(k * n * rows + d * w, 128), w)] = (jax.nn.silu(g) * u).astype(BF16)
 
         def gu_pumps(it):
-            @pl.when(jnp.logical_and(it >= 3, it < n_gu))
-            def _():
-                pump(base + 8 + it)
-
-            @pl.when(jnp.logical_or(it == 11, it == 14))
-            def _():
-                pump(base + 16 + (it - 11) // 3)
+            @pl.when(it < n_gu)
+            def _():
+                pump_span((7 + it, jnp.where(it < 4, 11, 7 + it)), (8 + it, jnp.where(it < 4, 11, 8 + it)))
         tiles(layer, first_gu, 2 * n_gu, (lambda it: lax.rem(it, n_gu), lambda it: it < n_gu), gu_compute, gu_pumps)
 
         def down_compute(it, slot):
@@ -334,10 +346,11 @@
                 send(p_out.at[:, cols], p_in.at[:, cols], sem_p.at[0, c], sem_p.at[1, c], pair)
 
         def down_pumps(it):
-            @pl.when(jnp.logical_or(it == 4, it == 6))
-            def _():
-                pump(base + 18 + (it - 4) // 2)
+            @pl.when(lax.rem(it, 2) == 0)
+            def _():
+                pump_span(15 + it // 2, 16 + it // 2)
         tiles(layer, first_down, 2 * n_down, (lambda it: it // 2, lambda it: lax.rem(it, 2) == 0), down_compute, down_pumps)
+        pump_span(19, 21)
         for c in range(n_down):
             for k in range(2):
                 arrive(p_in.at[:, pl.ds(c * 512, 512)], sem_p.at[k, c])

time: 787 us -> 713 us (0.906)
  Pallas kernels: 783 us -> 708 us
    pallas_call x1, Pallas kernels: 783 us -> 708 us  [local_fn(): pl.pallas_call(functools.partial(kernel, dims), out_shape=(jax.ShapeDtype...]
where the time goes in v3:
time: 713 us
  Pallas kernels  708 us (99%)
    pallas_call x1, Pallas kernels, local_fn(): pl.pallas_call(functools.partial(kernel, dims), out_shape=(jax.ShapeDtype...  708 us

profile of v3, /device:TPU:112, one launch (start us, length us, event | category | flops | bytes accessed | tf_op | source)
XLA Modules:
  0.0 712.6 jit_solution(14041764252209992403)
XLA Ops:
  0.0 1.3 maximum_convert_fusion.gains
  1.3 708.1 %shard_map.136 = (bf16[512,2048]{1,0:T(8,128)(2,1)}, bf16[34,8,256,1024]{3,2,1,0:T(8,128)(2,1)}) custom-call(bf16[512,2048]{1,0:T(8,128)(2,1)} %bitcast.2, f32[8,256]{1,0:T(8,128)} %maximum_convert_fusion.gains, f32[256,128]{1,0:T(8,128)} %constant.4.clone.cos_ref, f32[256,128]{1,0:T(8,128)} %constant.5.clone.sin_ref, bf16[2,256,2048]{2,1,0:T(8,128)(2,1)} %wq.1, ...), custom_call_target="tpu_custom_call" | custom-call | tf_op jit(solution)/shard_map/pallas_call | solution.py:393
  709.4 3.2 copy.16

commit v4 on v3

--- a/solution.py
+++ b/solution.py
@@ -163,7 +163,6 @@
 
     for s in range(AHEAD):
         start_own(jnp.int32(s))
-    x_copy = send(tokens, x2.at[pair_rows], sem_y.at[0], sem_y.at[1], pair)
     my_gain = gvec.at[:, pl.ds(pl.multiple_of(me * rows, 128), rows)]
     gain_copies = [send(gains, my_gain, sem_g.at[0], sem_g.at[1], {'fsdp': lax.rem(me + k, n)}) for k in range(1, n)]
     local = [pltpu.make_async_copy(tokens, x2.at[own_rows], sem_l.at[0]), pltpu.make_async_copy(gains, my_gain, sem_l.at[1])]
@@ -174,7 +173,6 @@
     gain_ref = gvec.at[:, pl.ds(0, (n - 1) * rows)]
     arrive(gain_ref, sem_g.at[0])
     arrive(gain_ref, sem_g.at[1])
-    x_copy.wait_send()
     for s in range(3):
         pump(jnp.int32(s))
 
@@ -207,11 +205,13 @@
                 return c
             lax.fori_loop(lo, hi, one, 0)
 
+        x_copy = send(x2.at[own_rows], x2.at[pair_rows], sem_y.at[0], sem_y.at[1], pair)
+
         def qkv_compute(it, slot):
             @pl.when(it == n_qkv)
             def _():
                 pump_span(5, (5, 7))
-                arrive(x2.at[pair_rows], sem_y.at[1])
+                x_copy.wait_recv()
             kind = lax.rem(it, n_qkv)
             r = pl.ds(pl.multiple_of((it // n_qkv) * n_tok, n_tok), n_tok)
             for k in range(SLAB // 512):
@@ -310,23 +310,42 @@
         h_copy = send(h2.at[own_rows], h2.at[pair_rows], sem_y.at[8], sem_y.at[9], pair)
         pump_span((7, 10), (7, 11))
 
-        def gu_compute(it, slot):
-            @pl.when(it == n_gu)
-            def _():
-                h_copy.wait()
-            d = lax.rem(it, n_gu)
-            r = pl.ds(pl.multiple_of((it // n_gu) * n_tok, n_tok), n_tok)
+        n_early = n_gu - 2
+
+        def gu_compute(d, theirs, slot):
+            r = pl.ds(pl.multiple_of(theirs * n_tok, n_tok), n_tok)
             for k in range(2):
                 w = ff_blk // 2
                 g = dot(h2[r, :], weight(slot, slice(k * w, (k + 1) * w))).astype(BF16).astype(F32)
                 u = dot(h2[r, :], weight(slot, slice(ff_blk + k * w, ff_blk + (k + 1) * w))).astype(BF16).astype(F32)
                 mid[r, pl.ds(pl.multiple_of(k * n * rows + d * w, 128), w)] = (jax.nn.silu(g) * u).astype(BF16)
 
-        def gu_pumps(it):
-            @pl.when(it < n_gu)
+        def gu_early(it, slot):
+            @pl.when(it == n_early)
+            def _():
+                h_copy.wait()
+            gu_compute(lax.rem(it, n_early), it // n_early, slot)
+
+        def early_pumps(it):
+            @pl.when(it < n_early)
             def _():
                 pump_span((7 + it, jnp.where(it < 4, 11, 7 + it)), (8 + it, jnp.where(it < 4, 11, 8 + it)))
-        tiles(layer, first_gu, 2 * n_gu, (lambda it: lax.rem(it, n_gu), lambda it: it < n_gu), gu_compute, gu_pumps)
+
+            @pl.when(it == n_early)
+            def _():
+                pump_span(13, (13, 14))
+        tiles(layer, first_gu, 2 * n_early, (lambda it: lax.rem(it, n_early), lambda it: it < n_early), gu_early, early_pumps)
+
+        def late_pumps(it):
+            @pl.when(it == 0)
+            def _():
+                pump_span((13, 14), 14)
+
+            @pl.when(it == 2)
+            def _():
+                pump_span(14, 15)
+        tiles(layer, first_gu + n_early, 2 * (n_gu - n_early), (lambda it: it // 2, lambda it: lax.rem(it, 2) == 0),
+              lambda it, slot: gu_compute(n_early + it // 2, lax.rem(it, 2), slot), late_pumps)
 
         def down_compute(it, slot):
             c = it // 2
@@ -354,11 +373,8 @@
         for c in range(n_down):
             for k in range(2):
                 arrive(p_in.at[:, pl.ds(c * 512, 512)], sem_p.at[k, c])
+        x_copy.wait_send()
         residual_norm(h2, lambda r: (p_own[r, :] + p_in[r, :]).astype(BF16).astype(F32), x2, 3 * n_layers + layer)
-
-        @pl.when(layer + 1 < n_layers)
-        def _():
-            send(x2.at[own_rows], x2.at[pair_rows], sem_y.at[0], sem_y.at[1], pair).wait_send()
         return carry
     lax.fori_loop(0, n_layers, layer_body, 0)
 

time: 713 us -> 665 us (0.933)
  Pallas kernels: 708 us -> 660 us
    pallas_call x1, Pallas kernels: 708 us -> 660 us  [local_fn(): pl.pallas_call(functools.partial(kernel, dims), out_shape=(jax.ShapeDtype...]
where the time goes in v4:
time: 665 us
  Pallas kernels  660 us (99%)
    pallas_call x1, Pallas kernels, local_fn(): pl.pallas_call(functools.partial(kernel, dims), out_shape=(jax.ShapeDtype...  660 us

profile of v4, /device:TPU:112, one launch (start us, length us, event | category | flops | bytes accessed | tf_op | source)
XLA Modules:
  0.0 664.7 jit_solution(9877867908039865536)
XLA Ops:
  0.0 1.3 maximum_convert_fusion.gains
  1.3 660.2 %shard_map.136 = (bf16[512,2048]{1,0:T(8,128)(2,1)}, bf16[34,8,256,1024]{3,2,1,0:T(8,128)(2,1)}) custom-call(bf16[512,2048]{1,0:T(8,128)(2,1)} %bitcast.2, f32[8,256]{1,0:T(8,128)} %maximum_convert_fusion.gains, f32[256,128]{1,0:T(8,128)} %constant.4.clone.cos_ref, f32[256,128]{1,0:T(8,128)} %constant.5.clone.sin_ref, bf16[2,256,2048]{2,1,0:T(8,128)(2,1)} %wq.1, ...), custom_call_target="tpu_custom_call" | custom-call | tf_op jit(solution)/shard_map/pallas_call | solution.py:409
  661.6 3.2 copy.16

commit v5 on v4

--- a/solution.py
+++ b/solution.py
@@ -13,7 +13,7 @@
 THETA = 500000.0
 SLAB = 1024
 AHEAD = 3
-LAG = 2
+TIGHT = 10
 F32 = jnp.float32
 BF16 = jnp.bfloat16
 
@@ -32,7 +32,7 @@
 
 def kernel(dims, tokens, gains, cos_ref, sin_ref, wq, wk, wv, wo, wg, wu, wd, out, gat,
            x2, qkv, att, att_in, alin, h2, mid, p_own, p_out, p_in, wbuf, stat, stat_in, gvec,
-           sem_a, sem_b, sem_c, sem_s, sem_w, sem_g, sem_y, sem_p, sem_l):
+           sem_a, sem_b, sem_c, sem_s, sem_w, sem_g, sem_y, sem_p, sem_o, sem_l):
     n, n_layers, n_tok, seq_len, width, rows, ff_blk, d_rows = dims
     half = width // 2
     n_heads = half // HEAD_DIM
@@ -60,6 +60,12 @@
     def arrive(ref, sem):
         pltpu.make_async_copy(ref, ref, sem).wait()
 
+    twin = first_out + 1
+
+    def out_block(layer, i):
+        first = 1 - (layer + n_layers - 1) // n_layers
+        return lax.rem(i + part * first, 2)
+
     def own_blocks(layer, pos, do):
         for i, w in enumerate((wq, wk, wv)):
             @pl.when(pos == i)
@@ -68,7 +74,7 @@
 
         @pl.when(jnp.logical_and(pos >= first_out, pos < first_gu))
         def _():
-            do(wo.at[layer, :, pl.ds(pl.multiple_of((pos - first_out) * SLAB, 128), SLAB)], slice(0, SLAB))
+            do(wo.at[layer, :, pl.ds(pl.multiple_of(out_block(layer, pos - first_out) * SLAB, 128), SLAB)], slice(0, SLAB))
 
         @pl.when(jnp.logical_and(pos >= first_gu, pos < first_down))
         def _():
@@ -85,13 +91,25 @@
     def start_own(s):
         def do(src, cols):
             dst = gat.at[s, me, :, cols]
-            send(src, dst, sem_s.at[s], sem_a.at[s], {'fsdp': right})
-            send(src, dst, sem_s.at[s], sem_a.at[s], {'fsdp': left})
+
+            @pl.when(jnp.logical_or(s < twin, s > twin))
+            def _():
+                send(src, dst, sem_s.at[s], sem_a.at[s], {'fsdp': right})
+                send(src, dst, sem_s.at[s], sem_a.at[s], {'fsdp': left})
             send(src, dst, sem_s.at[s], sem_c.at[s], {'fsdp': sib})
         own_blocks(s // per_layer, lax.rem(s, per_layer), do)
 
+    def to_twin(origin):
+        send(gat.at[twin - 1, origin], gat.at[twin, origin], sem_s.at[twin], sem_b.at[twin], pair)
+
+    def twin_relay():
+        arrive(gat.at[twin, pl.ds(0, 3)], sem_b.at[twin])
+        for origin in (left, right, far):
+            block = gat.at[twin, origin]
+            send(block, block, sem_s.at[twin], sem_c.at[twin], {'fsdp': sib})
+
     def pump(s):
-        @pl.when(s < n_stage)
+        @pl.when(jnp.logical_and(s < n_stage, jnp.logical_or(s < twin, s > twin)))
         def _():
             arrive(gat.at[s, pl.ds(0, 2)], sem_a.at[s])
             top, bottom = pl.ds(0, rows // 2), pl.ds(rows // 2, rows // 2)
@@ -103,16 +121,42 @@
                 block = gat.at[s, origin]
                 send(block, block, sem_s.at[s], sem_c.at[s], {'fsdp': sib})
 
-        @pl.when(s + AHEAD < n_stage)
-        def _():
-            start_own(s + AHEAD)
-
-        @pl.when(jnp.logical_and(s >= LAG, s < n_stage + LAG))
-        def _():
-            t = s - LAG
-            block = gat.at[t, far]
-            arrive(block, sem_b.at[t])
-            send(block, block, sem_s.at[t], sem_c.at[t], {'fsdp': sib})
+        @pl.when(s == twin - 1)
+        def _():
+            for origin in (left, right):
+                to_twin(origin)
+
+        pos = lax.rem(s, per_layer)
+        wrap = jnp.logical_and(pos == 0, s > 0)
+
+        def own(k, c):
+            t = s + AHEAD - 1 + k
+
+            @pl.when(jnp.logical_and(t < n_stage, jnp.logical_or(jnp.logical_and(k == 0, jnp.logical_or(pos > TIGHT, wrap)),
+                                                                 jnp.logical_and(k == 1, pos < TIGHT))))
+            def _():
+                start_own(t)
+            return c
+        lax.fori_loop(0, 2, own, 0)
+
+        def far_block(k, c):
+            t = s - 2 + k
+            two = jnp.logical_and(jnp.logical_and(s >= 2, s < n_stage), jnp.logical_and(pos <= TIGHT, jnp.logical_or(pos > 1, s < per_layer)))
+            one = jnp.logical_and(s <= n_stage, jnp.logical_or(pos >= TIGHT, wrap))
+
+            @pl.when(jnp.logical_or(jnp.logical_and(k == 0, two), jnp.logical_and(k == 1, one)))
+            def _():
+                @pl.when(jnp.logical_or(t < twin, t > twin))
+                def _():
+                    block = gat.at[t, far]
+                    arrive(block, sem_b.at[t])
+                    send(block, block, sem_s.at[t], sem_c.at[t], {'fsdp': sib})
+
+                @pl.when(t == twin - 1)
+                def _():
+                    to_twin(far)
+            return c
+        lax.fori_loop(0, 2, far_block, 0)
 
     def stage_ready(s):
         arrive(gat.at[s, pl.ds(0, 4)], sem_c.at[s])
@@ -138,19 +182,19 @@
                 stage_ready(layer * per_layer + pos)
             load(layer, pos, lax.rem(it, 2))
 
-        pumps(jnp.int32(0))
-        fetch(jnp.int32(0))
-
-        def body(it, carry):
-            @pl.when(it + 1 < count)
-            def _():
-                pumps(it + 1)
-                fetch(it + 1)
-            slot = lax.rem(it, 2)
-            loaded(slot)
-            compute(it, slot)
+        def body(step, carry):
+            @pl.when(step < count)
+            def _():
+                pumps(step)
+                fetch(step)
+
+            @pl.when(step > 0)
+            def _():
+                slot = lax.rem(step + 1, 2)
+                loaded(slot)
+                compute(step - 1, slot)
             return carry
-        lax.fori_loop(0, count, body, 0)
+        lax.fori_loop(0, count + 1, body, 0)
 
     def weight(slot, cols):
         return wbuf[slot, :, :, cols].reshape(n * rows, cols.stop - cols.start)
@@ -161,8 +205,11 @@
     pl.semaphore_signal(barrier, inc=1, device_id=pair, device_id_type=pl.DeviceIdType.MESH)
     pl.semaphore_wait(barrier, n)
 
-    for s in range(AHEAD):
-        start_own(jnp.int32(s))
+    def first_own(s, c):
+        start_own(s)
+        return c
+    lax.fori_loop(0, AHEAD, first_own, 0)
+    x_copy = send(tokens, x2.at[pair_rows], sem_y.at[0], sem_y.at[1], pair)
     my_gain = gvec.at[:, pl.ds(pl.multiple_of(me * rows, 128), rows)]
     gain_copies = [send(gains, my_gain, sem_g.at[0], sem_g.at[1], {'fsdp': lax.rem(me + k, n)}) for k in range(1, n)]
     local = [pltpu.make_async_copy(tokens, x2.at[own_rows], sem_l.at[0]), pltpu.make_async_copy(gains, my_gain, sem_l.at[1])]
@@ -173,8 +220,12 @@
     gain_ref = gvec.at[:, pl.ds(0, (n - 1) * rows)]
     arrive(gain_ref, sem_g.at[0])
     arrive(gain_ref, sem_g.at[1])
-    for s in range(3):
-        pump(jnp.int32(s))
+
+    def first_pump(s, c):
+        pump(s)
+        return c
+    lax.fori_loop(0, 3, first_pump, 0)
+    x_copy.wait_send()
 
     blk = 64
 
@@ -205,13 +256,11 @@
                 return c
             lax.fori_loop(lo, hi, one, 0)
 
-        x_copy = send(x2.at[own_rows], x2.at[pair_rows], sem_y.at[0], sem_y.at[1], pair)
-
         def qkv_compute(it, slot):
             @pl.when(it == n_qkv)
             def _():
                 pump_span(5, (5, 7))
-                x_copy.wait_recv()
+                arrive(x2.at[pair_rows], sem_y.at[1])
             kind = lax.rem(it, n_qkv)
             r = pl.ds(pl.multiple_of((it // n_qkv) * n_tok, n_tok), n_tok)
             for k in range(SLAB // 512):
@@ -235,13 +284,9 @@
                 stat[r, :] = jnp.where(lane < 64, stat[r, :], spread)
 
         def qkv_pumps(it):
-            @pl.when(it == 1)
-            def _():
-                pump_span((3, 4), 4)
-
-            @pl.when(it == 2)
-            def _():
-                pump_span(4, 5)
+            @pl.when(jnp.logical_and(it > 0, it < n_qkv))
+            def _():
+                pump_span((2 + it, 4), 3 + it)
         tiles(layer, 0, 2 * n_qkv, (lambda it: lax.rem(it, n_qkv), lambda it: it < n_qkv), qkv_compute, qkv_pumps)
 
         copies = [send(stat.at[own_rows], stat_in.at[pair_rows], sem_y.at[2], sem_y.at[3], pair),
@@ -278,22 +323,23 @@
                 return c2
             lax.fori_loop(0, n_heads, head, 0)
 
-            @pl.when(it == n_seq - 1)
-            def _():
-                send(att.at[pair_rows], att_in, sem_y.at[6], sem_y.at[7], pair)
-
-            @pl.when(it == 1)
-            def _():
-                pump_span((6, 8), (7, 9))
-
-            @pl.when(it == 3)
-            def _():
-                pump_span((7, 9), (7, 10))
+
+            @pl.when(it < n_seq)
+            def _():
+                send(att.at[r], att_in.at[pl.ds(pl.multiple_of(it * seq_len, seq_len), seq_len)], sem_o.at[0, it], sem_o.at[1, it], pair)
+
+            @pl.when(lax.rem(it, 2) == 1)
+            def _():
+                pump_span((6 + it // 2, 8 + it // 2), (7, 9 + it // 2))
             return carry
         lax.fori_loop(0, 2 * n_seq, attend, 0)
-        arrive(att_in, sem_y.at[6])
-        arrive(att_in, sem_y.at[7])
-
+        for i in range(n_seq):
+            for k in range(2):
+                arrive(att_in.at[pl.ds(i * seq_len, seq_len)], sem_o.at[k, i])
+
+        @pl.when(layer == 0)
+        def _():
+            twin_relay()
         def out_compute(it, slot):
             q = n // 2
             for k in range(SLAB // 512):
@@ -301,7 +347,7 @@
                 w_mine = wbuf[slot, pl.ds(part * q, q), :, cols].reshape(q * rows, 512)
                 w_theirs = wbuf[slot, pl.ds((1 - part) * q, q), :, cols].reshape(q * rows, 512)
                 val = dot(att[own_rows, :], w_mine) + dot(att_in[...], w_theirs)
-                alin[:, pl.ds(pl.multiple_of(it * SLAB + k * 512, 128), 512)] = val.astype(BF16)
+                alin[:, pl.ds(pl.multiple_of(out_block(layer, it) * SLAB + k * 512, 128), 512)] = val.astype(BF16)
 
         def out_pumps(it):
             return
@@ -327,23 +373,19 @@
             gu_compute(lax.rem(it, n_early), it // n_early, slot)
 
         def early_pumps(it):
-            @pl.when(it < n_early)
-            def _():
-                pump_span((7 + it, jnp.where(it < 4, 11, 7 + it)), (8 + it, jnp.where(it < 4, 11, 8 + it)))
-
-            @pl.when(it == n_early)
-            def _():
-                pump_span(13, (13, 14))
+            @pl.when(it < 4)
+            def _():
+                pump_span((7 + it, 11), (8 + it, 11))
+
+            @pl.when(jnp.logical_or(it == 5, it == 6))
+            def _():
+                pump_span(6 + it, (12, 7 + it))
         tiles(layer, first_gu, 2 * n_early, (lambda it: lax.rem(it, n_early), lambda it: it < n_early), gu_early, early_pumps)
 
         def late_pumps(it):
-            @pl.when(it == 0)
-            def _():
-                pump_span((13, 14), 14)
-
-            @pl.when(it == 2)
-            def _():
-                pump_span(14, 15)
+            @pl.when(lax.rem(it, 2) == 0)
+            def _():
+                pump_span((12 + it // 2, 13), 13 + it // 2)
         tiles(layer, first_gu + n_early, 2 * (n_gu - n_early), (lambda it: it // 2, lambda it: lax.rem(it, 2) == 0),
               lambda it, slot: gu_compute(n_early + it // 2, lax.rem(it, 2), slot), late_pumps)
 
@@ -367,14 +409,20 @@
         def down_pumps(it):
             @pl.when(lax.rem(it, 2) == 0)
             def _():
-                pump_span(15 + it // 2, 16 + it // 2)
+                pump_span(14 + it // 2, 15 + it // 2)
         tiles(layer, first_down, 2 * n_down, (lambda it: it // 2, lambda it: lax.rem(it, 2) == 0), down_compute, down_pumps)
-        pump_span(19, 21)
+        pump_span(18, 21)
         for c in range(n_down):
             for k in range(2):
                 arrive(p_in.at[:, pl.ds(c * 512, 512)], sem_p.at[k, c])
-        x_copy.wait_send()
+        @pl.when(layer > 0)
+        def _():
+            arrive(x2.at[own_rows], sem_y.at[0])
         residual_norm(h2, lambda r: (p_own[r, :] + p_in[r, :]).astype(BF16).astype(F32), x2, 3 * n_layers + layer)
+
+        @pl.when(layer + 1 < n_layers)
+        def _():
+            send(x2.at[own_rows], x2.at[pair_rows], sem_y.at[0], sem_y.at[1], pair)
         return carry
     lax.fori_loop(0, n_layers, layer_body, 0)
 
@@ -434,6 +482,7 @@
                 pltpu.SemaphoreType.DMA((2,)),
                 pltpu.SemaphoreType.DMA((10,)),
                 pltpu.SemaphoreType.DMA((2, width // 512)),
+                pltpu.SemaphoreType.DMA((2, n_seq)),
                 pltpu.SemaphoreType.DMA((2,)),
             ],
             compiler_params=pltpu.CompilerParams(collective_id=0, has_side_effects=True, vmem_limit_bytes=62 * 1024 * 1024),

time: 665 us -> 644 us (0.968)
  Pallas kernels: 660 us -> 639 us
    pallas_call x1, Pallas kernels: 660 us -> 639 us  [local_fn(): pl.pallas_call(functools.partial(kernel, dims), out_shape=(jax.ShapeDtype...]
where the time goes in v5:
time: 644 us; the launch traced here: 643 us
  Pallas kernels  639 us (99%)
    pallas_call x1, Pallas kernels, local_fn(): pl.pallas_call(functools.partial(kernel, dims), out_shape=(jax.ShapeDtype...  639 us

profile of v5, /device:TPU:112, one launch (start us, length us, event | category | flops | bytes accessed | tf_op | source)
XLA Modules:
  0.0 643.1 jit_solution(13836738928577490734)
XLA Ops:
  0.0 1.3 maximum_convert_fusion.gains
  1.3 638.6 %shard_map.136 = (bf16[512,2048]{1,0:T(8,128)(2,1)}, bf16[34,8,256,1024]{3,2,1,0:T(8,128)(2,1)}) custom-call(bf16[512,2048]{1,0:T(8,128)(2,1)} %bitcast.2, f32[8,256]{1,0:T(8,128)} %maximum_convert_fusion.gains, f32[256,128]{1,0:T(8,128)} %constant.4.clone.cos_ref, f32[256,128]{1,0:T(8,128)} %constant.5.clone.sin_ref, bf16[2,256,2048]{2,1,0:T(8,128)(2,1)} %wq.1, ...), custom_call_target="tpu_custom_call" | custom-call | tf_op jit(solution)/shard_map/pallas_call | solution.py:457
  640.0 3.2 copy.16

commit v6 on v5

--- a/solution.py
+++ b/solution.py
@@ -171,7 +171,7 @@
     def loaded(slot):
         arrive(wbuf.at[slot], sem_w.at[slot])
 
-    def tiles(layer, first, count, repeat, compute, pumps):
+    def tiles(layer, first, count, repeat, compute, pumps, paced=False):
         stage, fresh = repeat
 
         def fetch(it):
@@ -183,16 +183,23 @@
             load(layer, pos, lax.rem(it, 2))
 
         def body(step, carry):
-            @pl.when(step < count)
-            def _():
-                pumps(step)
-                fetch(step)
+            def ahead():
+                @pl.when(step < count)
+                def _():
+                    pumps(step)
+                    fetch(step)
+
+            if not paced:
+                ahead()
 
             @pl.when(step > 0)
             def _():
                 slot = lax.rem(step + 1, 2)
                 loaded(slot)
                 compute(step - 1, slot)
+
+            if paced:
+                ahead()
             return carry
         lax.fori_loop(0, count + 1, body, 0)
 
@@ -291,7 +298,7 @@
 
         copies = [send(stat.at[own_rows], stat_in.at[pair_rows], sem_y.at[2], sem_y.at[3], pair),
                   send(stat.at[pair_rows], stat_in.at[own_rows], sem_y.at[4], sem_y.at[5], pair)]
-        pump_span((5, 7), (6, 8))
+        pump_span((5, 7), (7, 8))
         for c in copies:
             c.wait()
 
@@ -330,7 +337,7 @@
 
             @pl.when(lax.rem(it, 2) == 1)
             def _():
-                pump_span((6 + it // 2, 8 + it // 2), (7, 9 + it // 2))
+                pump_span((7 + it // 2, 8 + it // 2), (8 + it // 2, 9 + it // 2))
             return carry
         lax.fori_loop(0, 2 * n_seq, attend, 0)
         for i in range(n_seq):
@@ -354,7 +361,7 @@
         tiles(layer, first_out, n_out, (lambda it: it, lambda it: it >= 0), out_compute, out_pumps)
         residual_norm(x2, lambda r: alin[r, :].astype(F32), h2, 2 * n_layers + layer)
         h_copy = send(h2.at[own_rows], h2.at[pair_rows], sem_y.at[8], sem_y.at[9], pair)
-        pump_span((7, 10), (7, 11))
+        pump_span((9, 10), (9, 11))
 
         n_early = n_gu - 2
 
@@ -373,44 +380,45 @@
             gu_compute(lax.rem(it, n_early), it // n_early, slot)
 
         def early_pumps(it):
-            @pl.when(it < 4)
-            def _():
-                pump_span((7 + it, 11), (8 + it, 11))
-
-            @pl.when(jnp.logical_or(it == 5, it == 6))
-            def _():
-                pump_span(6 + it, (12, 7 + it))
+            @pl.when(jnp.logical_and(it >= 2, it < 4))
+            def _():
+                pump_span((7 + it, 9 + it), (8 + it, 12))
+
+            @pl.when(it == 5)
+            def _():
+                pump_span((11, 12), (12, 13))
+
+            @pl.when(it == 10)
+            def _():
+                pump_span((12, 13), (12, 14))
         tiles(layer, first_gu, 2 * n_early, (lambda it: lax.rem(it, n_early), lambda it: it < n_early), gu_early, early_pumps)
 
         def late_pumps(it):
-            @pl.when(lax.rem(it, 2) == 0)
-            def _():
-                pump_span((12 + it // 2, 13), 13 + it // 2)
-        tiles(layer, first_gu + n_early, 2 * (n_gu - n_early), (lambda it: it // 2, lambda it: lax.rem(it, 2) == 0),
-              lambda it, slot: gu_compute(n_early + it // 2, lax.rem(it, 2), slot), late_pumps)
-
-        def down_compute(it, slot):
-            c = it // 2
-            cols = pl.ds(pl.multiple_of(c * 512, 512), 512)
-            mine = lax.rem(it, 2)
-            r = pl.ds(pl.multiple_of((1 - mine) * n_tok, n_tok), n_tok)
+            pump_span((12 + it, 14), (13 + it, 14))
+        tiles(layer, first_gu + n_early, n_gu - n_early, (lambda it: it, lambda it: it >= 0),
+              lambda it, slot: gu_compute(n_early + it, 1, slot), late_pumps, paced=True)
+
+        def down_dot(c, r, slot):
             k_half = n * rows
-            val = dot(mid[r, 0:k_half], weight(slot, slice(0, 512))) + dot(mid[r, k_half:2 * k_half], weight(slot, slice(512, 1024)))
-
-            @pl.when(mine == 1)
-            def _():
-                p_own[:, cols] = val
-
-            @pl.when(mine == 0)
-            def _():
-                p_out[:, cols] = val
-                send(p_out.at[:, cols], p_in.at[:, cols], sem_p.at[0, c], sem_p.at[1, c], pair)
+            return dot(mid[r, 0:k_half], weight(slot, slice(0, 512))) + dot(mid[r, k_half:2 * k_half], weight(slot, slice(512, 1024)))
+
+        def down_pair(it, slot):
+            cols = pl.ds(pl.multiple_of(it * 512, 512), 512)
+            p_out[:, cols] = down_dot(it, pair_rows, slot)
+            send(p_out.at[:, cols], p_in.at[:, cols], sem_p.at[0, it], sem_p.at[1, it], pair)
 
         def down_pumps(it):
-            @pl.when(lax.rem(it, 2) == 0)
-            def _():
-                pump_span(14 + it // 2, 15 + it // 2)
-        tiles(layer, first_down, 2 * n_down, (lambda it: it // 2, lambda it: lax.rem(it, 2) == 0), down_compute, down_pumps)
+            pump_span(14 + it, 15 + it)
+        tiles(layer, first_down, n_down, (lambda it: it, lambda it: it >= 0), down_pair, down_pumps, paced=True)
+
+        def no_pumps(it):
+            pass
+        tiles(layer, first_gu + n_early, n_gu - n_early, (lambda it: it, lambda it: it < 0),
+              lambda it, slot: gu_compute(n_early + it, 0, slot), no_pumps)
+
+        def down_own(it, slot):
+            p_own[:, pl.ds(pl.multiple_of(it * 512, 512), 512)] = down_dot(it, own_rows, slot)
+        tiles(layer, first_down, n_down, (lambda it: it, lambda it: it < 0), down_own, no_pumps)
         pump_span(18, 21)
         for c in range(n_down):
             for k in range(2):

time: 644 us -> 644 us (level)
  no operation moved by 1% of the time
where the time goes in v6:
time: 644 us
  Pallas kernels  639 us (99%)
    pallas_call x1, Pallas kernels, local_fn(): pl.pallas_call(functools.partial(kernel, dims), out_shape=(jax.ShapeDtype...  639 us

profile of v6, /device:TPU:112, one launch (start us, length us, event | category | flops | bytes accessed | tf_op | source)
XLA Modules:
  0.0 643.5 jit_solution(145457016671488290)
XLA Ops:
  0.0 1.3 maximum_convert_fusion.gains
  1.3 639.0 %shard_map.136 = (bf16[512,2048]{1,0:T(8,128)(2,1)}, bf16[34,8,256,1024]{3,2,1,0:T(8,128)(2,1)}) custom-call(bf16[512,2048]{1,0:T(8,128)(2,1)} %bitcast.2, f32[8,256]{1,0:T(8,128)} %maximum_convert_fusion.gains, f32[256,128]{1,0:T(8,128)} %constant.4.clone.cos_ref, f32[256,128]{1,0:T(8,128)} %constant.5.clone.sin_ref, bf16[2,256,2048]{2,1,0:T(8,128)(2,1)} %wq.1, ...), custom_call_target="tpu_custom_call" | custom-call | tf_op jit(solution)/shard_map/pallas_call | solution.py:465
  640.4 3.2 copy.16
